TPU v7x, 256 devices: a 8x8x2 block of a 8x8x16 slice. The times are simulated.
256 devices in a mesh: grp: 2 (over z), row: 16 (over x, core), sub: 8 (over y).
Axes of the slice: x: 8, y: 8, z: 2, core: 2. Of those that a mesh axis runs over, the one named last changes fastest.
The devices are a block of a 8x8x16 slice.
Arguments:
- residual_in: float32 [4, 2048, 2048], P('grp', ('row', 'sub')), parts along dimension 0, may hold values from -100 to 100
- direction: float32 [4, 2048, 2048], P('grp', ('row', 'sub')), parts along dimension 0, may hold values from -100 to 100
- spectrum: float32 [8192, 4096], P('grp', ('row', 'sub')), parts along dimension 0, may hold values from 0.0999 to 10.001, as said below
- noise_var: float32 [2], P('grp'), parts along dimension 0, may hold values from 0.5 to 2
Outputs:
- residual_out: float32 [4, 2048, 2048], P('grp', ('row', 'sub')), parts along dimension 0
- direction_out: float32 [4, 2048, 2048], P('grp', ('row', 'sub')), parts along dimension 0
- step_size: float32 [4], P('grp'), parts along dimension 0
There are 2 independent parts, one for each index of `grp`. A program takes and returns all parts, laid end to end along the dimension named above; each array names one. Nothing has to cross between parts.
Inputs may be any that keep to these rules, and one draw needn't show every extreme that they name: spectrum[k, l] = spectrum[(4096 - k) % 4096, (4096 - l) % 4096] for all k, l.
All inputs are finite; a program needn't handle non-finite values.
Results may differ from a plain program's by a relative error of at most 0.00005.
Values sent between devices are 32-bit elements; how exact they have to be, the bound alone decides.
A program may use at most 64 MiB of HBM per device.

v0:
```python
import functools
import math

import jax
import jax.numpy as jnp
from jax import lax
from jax.sharding import Mesh
from jax.sharding import PartitionSpec as P

ROW = ("row_0", "row_1")
ROW_SUB = ("row_0", "row_1", "sub")


high_factor = 128
tiny_value = 1e-06


def split_up(value, dim, count):
    dims = value.shape
    parts = value.reshape(*dims[:dim], count, dims[dim] // count, *dims[dim + 1 :])
    return jnp.moveaxis(parts, dim, 0)


def edges_of(length, count):
    hop = length // count
    if hop >= 8:
        hop -= hop % 8
    return [hop * k for k in range(1, count)]


def laid_out(parts, dim):
    dims = list(parts.shape[1:])
    dims[dim] *= parts.shape[0]
    return jnp.moveaxis(parts, 0, dim).reshape(dims)


def exchange_in_pieces(value, axis, pieces, split_dim, concat_dim):
    parts = split_up(value, split_dim, lax.axis_size(axis))
    cut = max(range(1, max(2, parts.ndim - 1)), key=lambda d: parts.shape[d])
    finished = []
    for share in jnp.split(parts, edges_of(parts.shape[cut], pieces), axis=cut):
        if share.size:
            finished.append(lax.all_to_all(share, axis, split_axis=0, concat_axis=0, tiled=True))
    return laid_out(jnp.concatenate(finished, axis=cut), concat_dim)


def over_axes(value, axes):
    return functools.reduce(lax.psum, axes, value)


def phase_pair(left_ids, right_ids, modulus, orient):
    turns = left_ids * right_ids % modulus
    angle = orient * 2.0 * math.pi / modulus * turns.astype(jnp.float32)
    return (jnp.cos(angle), jnp.sin(angle))


def complex_table(cos_part, sin_part):
    upper_rows = jnp.stack([cos_part, sin_part], axis=1)
    lower_rows = jnp.stack([-sin_part, cos_part], axis=1)
    return jnp.stack([upper_rows, lower_rows], axis=1)


def rotate(values, cos_part, sin_part, at_axis):
    real_part = lax.index_in_dim(values, 0, at_axis, keepdims=False)
    imag_part = lax.index_in_dim(values, 1, at_axis, keepdims=False)
    return jnp.stack(
        [real_part * cos_part - imag_part * sin_part, real_part * sin_part + imag_part * cos_part],
        axis=at_axis,
    )


def contract(form_spec, operand, table_arr):
    return jnp.einsum(form_spec, operand, table_arr, precision=lax.Precision.HIGHEST)


def body(residual_in, direction, spectrum, noise_var):
    probes, rows_dev, grid_len = direction.shape
    embed_len = 2 * grid_len
    low_factor = embed_len // high_factor
    half_factor = grid_len // high_factor
    n_row = lax.axis_size(ROW)
    n_sub = lax.axis_size("sub")
    devices = n_row * n_sub
    per_device = high_factor // devices
    slot_ids = jnp.arange(high_factor, dtype=jnp.int32)
    first_ids = jnp.arange(half_factor, dtype=jnp.int32)
    second_ids = jnp.arange(low_factor, dtype=jnp.int32)
    short_cos, short_sin = phase_pair(first_ids[:, None], second_ids[None, :], low_factor, -1.0)
    turn_cos, turn_sin = phase_pair(slot_ids[:, None], second_ids[None, :], embed_len, -1.0)
    long_cos, long_sin = phase_pair(slot_ids[:, None], slot_ids[None, :], high_factor, -1.0)
    plain_cos, plain_sin = phase_pair(slot_ids[:, None], slot_ids[None, :], high_factor, -1.0)
    back_cos, back_sin = phase_pair(slot_ids[:, None], slot_ids[None, :], high_factor, 1.0)
    perm_cos, perm_sin = phase_pair(slot_ids[:, None], slot_ids[None, :], high_factor, 1.0)
    last_cos, last_sin = phase_pair(second_ids[:, None], first_ids[None, :], low_factor, 1.0)
    fields = direction.reshape(probes // 2, 2, rows_dev, half_factor, high_factor)
    spread = contract("ycrab,acdm->yrbdm", fields, complex_table(short_cos, short_sin))
    batches = spread.shape[0]
    spread = rotate(spread, turn_cos, turn_sin, 3)
    row_freq = contract("frbcm,bcdk->frkdm", spread, complex_table(long_cos, long_sin))
    row_freq = row_freq.reshape(batches, rows_dev, 2 * embed_len)
    columns = exchange_in_pieces(row_freq, ROW_SUB, 2, 2, 1)
    columns = columns.reshape(batches, half_factor, high_factor, per_device, 2, low_factor)
    turned = contract("fabqcm,acdj->fjbqdm", columns, complex_table(short_cos, short_sin))
    turned = rotate(turned, turn_cos.T[:, :, None, None], turn_sin.T[:, :, None, None], 4)
    spectra = contract("fjbqcm,bcdk->fkjqdm", turned, complex_table(plain_cos, plain_sin))
    weights = (spectrum * (1.0 / (embed_len * embed_len))).reshape(
        high_factor, low_factor, per_device, low_factor
    )
    spectra = spectra * weights[None, :, :, :, None, :]
    inverted = contract("fkjqcm,kcdb->fbjqdm", spectra, complex_table(back_cos, back_sin))
    inverted = rotate(inverted, turn_cos[:, :, None, None], -turn_sin[:, :, None, None], 4)
    grid_cols = contract("fbjqcm,jcda->fabqdm", inverted, complex_table(last_cos, last_sin))
    grid_cols = grid_cols.reshape(batches, grid_len, 2 * embed_len // devices)
    rows_back = lax.all_to_all(grid_cols, ROW_SUB, split_axis=1, concat_axis=2, tiled=True)
    rows_back = rows_back.reshape(batches, rows_dev, high_factor, 2, low_factor)
    mixed = contract("frkcm,kcdb->frbdm", rows_back, complex_table(perm_cos, perm_sin))
    mixed = rotate(mixed, turn_cos, -turn_sin, 3)
    applied = contract("frbcm,mcda->fdrab", mixed, complex_table(last_cos, last_sin))
    applied = applied.reshape(probes, rows_dev, grid_len)
    image_out = applied + noise_var[0] * direction
    own_curv = jnp.sum(direction * image_out, axis=(1, 2))
    own_norm = jnp.sum(residual_in * residual_in, axis=(1, 2))
    old_norm, curvature = (over_axes(own_norm, ROW_SUB), over_axes(own_curv, ROW_SUB))
    step_size = old_norm / curvature
    residual_out = residual_in - step_size[:, None, None] * image_out
    new_norm = over_axes(jnp.sum(residual_out * residual_out, axis=(1, 2)), ROW_SUB)
    direction_out = residual_out + (new_norm / (old_norm + tiny_value))[:, None, None] * direction
    return (residual_out, direction_out, step_size)


def solution(mesh):
    torus = Mesh(
        mesh.devices.reshape(mesh.shape["grp"], 8, 2, mesh.shape["sub"]),
        ("grp", "row_0", "row_1", "sub"),
    )
    in_specs = (P("grp", ROW_SUB, None), P("grp", ROW_SUB, None), P("grp", ROW_SUB), P("grp"))
    out_specs = (P("grp", ROW_SUB, None), P("grp", ROW_SUB, None), P("grp"))
    return jax.shard_map(body, mesh=torus, in_specs=in_specs, out_specs=out_specs, check_vma=False)
```

profile of v0, /device:TPU:513, one launch (start us, length us, event | category | flops | bytes accessed | tf_op | source)
XLA Modules:
  0.0 185.9 jit_solution(11520293836639985032)
XLA Ops:
  0.7 0.1 fusion.58
  0.8 0.1 fusion.44
  0.8 0.3 multiply_sine_fusion
  1.1 0.3 fusion.23
  1.4 1.0 copy.72
  2.4 0.6 convolution_bitcast_fusion.5
  3.1 0.1 multiply_subtract_fusion.4
  3.2 0.6 convolution_bitcast_fusion.4
  3.9 0.2 copy.44
  4.1 1.0 reshape.538
  5.2 27.6 %all-to-all-start.1 = ((f32[128,1,512]{2,1,0:T(1,128)}), f32[128,1,512]{2,1,0:T(1,128)S(1)}, u32[]{:S(2)}, u32[]{:S(2)}) async-start(f32[128,1,512]{2,1,0:T(1,128)} %reshape.538), calls=%async_computation.1 | async-start | bytes 524288 | tf_op jit(solution)/shard_map/all_to_all | solution.py:43
  32.8 0.2 copy.43
  33.0 1.0 reshape.540
  34.1 0.7 mul.760
  34.8 1.5 copy.47
  36.2 0.7 fusion.52
  37.0 0.7 fusion.42
  37.7 9.4 %all-to-all-done.1 = f32[128,1,512]{2,1,0:T(1,128)S(1)} async-done(((f32[128,1,512]{2,1,0:T(1,128)}), f32[128,1,512]{2,1,0:T(1,128)S(1)}, u32[]{:S(2)}, u32[]{:S(2)}) %all-to-all-start.1) | async-done | bytes 262176 | tf_op jit(solution)/shard_map/all_to_all | solution.py:43
  47.1 7.6 %all-to-all-start = ((f32[128,1,512]{2,1,0:T(1,128)}), f32[128,1,512]{2,1,0:T(1,128)S(1)}, u32[]{:S(2)}, u32[]{:S(2)}) async-start(f32[128,1,512]{2,1,0:T(1,128)} %reshape.540), calls=%async_computation | async-start | bytes 524288 | tf_op jit(solution)/shard_map/all_to_all | solution.py:43
  54.8 0.6 maximum_bitcast_fusion.18
  55.4 0.3 fusion.22
  55.7 0.3 multiply_sine_fusion.1
  56.0 0.7 maximum_bitcast_fusion.8
  56.6 0.5 broadcast.730
  57.1 1.3 reduce
  58.4 0.1 reshape.539
  58.5 10.1 %all-to-all-done = f32[128,1,512]{2,1,0:T(1,128)S(1)} async-done(((f32[128,1,512]{2,1,0:T(1,128)}), f32[128,1,512]{2,1,0:T(1,128)S(1)}, u32[]{:S(2)}, u32[]{:S(2)}) %all-to-all-start) | async-done | bytes 262176 | tf_op jit(solution)/shard_map/all_to_all | solution.py:43
  68.6 1.3 reduce.1
  69.9 0.1 reshape.541
  70.0 0.1 pad_maximum_fusion
  70.1 1.2 reshape.509
  71.3 0.9 copy.45
  72.2 1.0 convolution_bitcast_fusion
  73.3 0.2 multiply_subtract_fusion.1
  73.4 0.1 maximum_bitcast_fusion
  73.5 0.8 copy-done.1
  74.3 1.7 fusion.1
  76.0 1.0 convolution_bitcast_fusion.1
  77.0 0.2 multiply_subtract_fusion
  77.2 0.1 maximum_bitcast_fusion.1
  77.3 0.4 copy-done.7
  77.7 1.2 convolution_bitcast_fusion.6
  79.0 0.1 reshape.513
  79.1 0.6 copy.51
  79.7 9.6 %reduce.2 = f32[2048,64]{1,0:T(8,128)S(1)} reduce(f32[2048,1,64]{2,1,0:T(1,128)S(1)} %bitcast.174, f32[]{:T(128)} %broadcast.730), dimensions={1}, to_apply=%bitcast.155.reduce_sub_computation | reduce | bytes 1048580
  89.3 1.4 reshape.542
  90.8 7.7 %all-to-all-start.2 = ((f32[128,1,1024]{2,1,0:T(1,128)}), f32[128,1,1024]{2,1,0:T(1,128)S(1)}, u32[]{:S(2)}, u32[]{:S(2)}) async-start(f32[128,1,1024]{2,1,0:T(1,128)} %reshape.542), calls=%async_computation.2 | async-start | bytes 1048576 | tf_op jit(solution)/shard_map/all_to_all | solution.py:114
  99.1 0.1 multiply_reduce_fusion.2
  99.3 18.6 %all-to-all-done.2 = f32[128,1,1024]{2,1,0:T(1,128)S(1)} async-done(((f32[128,1,1024]{2,1,0:T(1,128)}), f32[128,1,1024]{2,1,0:T(1,128)S(1)}, u32[]{:S(2)}, u32[]{:S(2)}) %all-to-all-start.2) | async-done | bytes 524320 | tf_op jit(solution)/shard_map/all_to_all | solution.py:114
  117.8 1.9 %reduce.3 = f32[128,1024]{1,0:T(8,128)S(1)} reduce(f32[128,1,1024]{2,1,0:T(1,128)S(1)} %all-to-all-done.2, f32[]{:T(128)} %broadcast.730), dimensions={1}, to_apply=%all_to_all.19.reduce_sub_computation | reduce | bytes 1048580 | tf_op jit(solution)/shard_map/all_to_all | solution.py:114
  119.7 1.3 reshape.543
  121.0 0.4 copy.52
  121.5 0.6 convolution_bitcast_fusion.3
  122.1 0.1 multiply_subtract_fusion.3
  122.2 0.4 convolution_bitcast_fusion.7
  122.6 0.1 multiply_reduce_fusion.1
  122.8 11.4 %all-reduce.1 = (f32[2]{0:T(128)S(1)}, f32[2]{0:T(128)S(1)}) all-reduce(f32[2]{0:T(128)S(1)} %multiply_reduce_fusion.2, f32[2]{0:T(128)S(1)} %multiply_reduce_fusion.1), channel_id=1, replica_groups=mesh['grp'=2,'row_0'=8,'row_1'=2,'sub'=8] {'row_0'}, use_global_device_ids=true, to_apply=%region_1.2 | all-reduce | flops 4 | bytes 32 | tf_op jit(solution)/shard_map/psum | solution.py:48
  134.2 5.5 %all-reduce.2 = (f32[2]{0:T(128)S(1)}, f32[2]{0:T(128)S(1)}) all-reduce(f32[2]{0:T(128)S(1)} %get-tuple-element.5, f32[2]{0:T(128)S(1)} %get-tuple-element.6), channel_id=1, replica_groups=mesh['grp'=2,'row_0'=8,'row_1'=2,'sub'=8] {'row_1'}, use_global_device_ids=true, to_apply=%region_2.3 | all-reduce | flops 4 | bytes 32 | tf_op jit(solution)/shard_map/psum | solution.py:48
  139.8 13.0 %all-reduce = (f32[2]{0:T(128)S(1)}, f32[2]{0:T(128)S(1)}) all-reduce(f32[2]{0:T(128)S(1)} %get-tuple-element.7, f32[2]{0:T(128)S(1)} %get-tuple-element.8), channel_id=1, replica_groups=mesh['grp'=2,'row_0'=8,'row_1'=2,'sub'=8] {'sub'}, use_global_device_ids=true, to_apply=%region_3.4 | all-reduce | flops 4 | bytes 32 | tf_op jit(solution)/shard_map/psum | solution.py:48
  152.7 0.2 multiply_reduce_fusion
  152.9 11.5 %psum.69 = f32[2]{0:T(128)S(1)} all-reduce(f32[2]{0:T(128)S(1)} %get-tuple-element.9), channel_id=1, replica_groups=mesh['grp'=2,'row_0'=8,'row_1'=2,'sub'=8] {'row_0'}, use_global_device_ids=true, to_apply=%region_9.10 | all-reduce | flops 2 | bytes 16 | tf_op jit(solution)/shard_map/psum | solution.py:48
  164.5 9.8 %psum.70 = f32[2]{0:T(128)S(1)} all-reduce(f32[2]{0:T(128)S(1)} %psum.69), channel_id=1, replica_groups=mesh['grp'=2,'row_0'=8,'row_1'=2,'sub'=8] {'row_1'}, use_global_device_ids=true, to_apply=%region_10.11 | all-reduce | flops 2 | bytes 16 | tf_op jit(solution)/shard_map/psum | solution.py:48
  174.3 10.8 %psum.71 = f32[2]{0:T(128)S(1)} all-reduce(f32[2]{0:T(128)S(1)} %psum.70), channel_id=1, replica_groups=mesh['grp'=2,'row_0'=8,'row_1'=2,'sub'=8] {'sub'}, use_global_device_ids=true, to_apply=%region_11.12 | all-reduce | flops 2 | bytes 16 | tf_op jit(solution)/shard_map/psum | solution.py:48
  185.1 0.8 multiply_add_fusion.2
  (41 shorter events, 0.5 us)
Async XLA Ops:
  2.4 0.7 copy-start.9
  2.4 0.7 copy-start.11
  3.8 29.0 %copy-start.5 = (f32[4096,32]{0,1:T(8,128)S(1)}, f32[4096,32]{0,1:T(8,128)}, u32[]{:S(2)}) copy-start(f32[4096,32]{0,1:T(8,128)} %param.6) | copy-start | bytes 1572868
  5.2 41.9 %all-to-all-start.1 = ((f32[128,1,512]{2,1,0:T(1,128)}), f32[128,1,512]{2,1,0:T(1,128)S(1)}, u32[]{:S(2)}, u32[]{:S(2)}) async-start(f32[128,1,512]{2,1,0:T(1,128)} %reshape.538), calls=%async_computation.1 | async-start | bytes 524288 | tf_op jit(solution)/shard_map/all_to_all | solution.py:43
  47.1 21.5 %all-to-all-start = ((f32[128,1,512]{2,1,0:T(1,128)}), f32[128,1,512]{2,1,0:T(1,128)S(1)}, u32[]{:S(2)}, u32[]{:S(2)}) async-start(f32[128,1,512]{2,1,0:T(1,128)} %reshape.540), calls=%async_computation | async-start | bytes 524288 | tf_op jit(solution)/shard_map/all_to_all | solution.py:43
  71.3 0.9 copy-start.10
  71.3 0.9 copy-start.12
  71.3 1.9 %copy-start.13 = (f32[32,128]{1,0:T(8,128)S(1)}, f32[32,128]{1,0:T(8,128)}, u32[]{:S(2)}) copy-start(f32[32,128]{1,0:T(8,128)} %get-tuple-element.35) | copy-start | bytes 49156
  71.3 1.9 %copy-start.14 = (f32[32,128]{1,0:T(8,128)S(1)}, f32[32,128]{1,0:T(8,128)}, u32[]{:S(2)}) copy-start(f32[32,128]{1,0:T(8,128)} %get-tuple-element.36) | copy-start | bytes 49156
  73.2 1.0 copy-start.1
  73.4 2.6 %copy-start.2 = (f32[128,1,2,128]{3,0,2,1:T(8,128)S(1)}, f32[128,1,2,128]{3,0,2,1:T(8,128)}, u32[]{:S(2)}) copy-start(f32[128,1,2,128]{3,0,2,1:T(8,128)} %get-tuple-element.22) | copy-start | bytes 393220
  74.3 2.7 %copy-start.6 = (f32[128,32]{0,1:T(8,128)S(1)}, f32[128,32]{0,1:T(8,128)}, u32[]{:S(2)}) copy-start(f32[128,32]{0,1:T(8,128)} %fusion.52) | copy-start | bytes 49156
  77.0 0.7 copy-start.7
  77.0 0.7 copy-start.8
  79.7 19.4 %copy-start.3 = (f32[2,16,2048]{2,1,0:T(8,128)S(1)}, f32[2,16,2048]{2,1,0:T(8,128)}, u32[]{:S(2)}) copy-start(f32[2,16,2048]{2,1,0:T(8,128)} %param.4) | copy-start | bytes 786436
  90.8 27.1 %all-to-all-start.2 = ((f32[128,1,1024]{2,1,0:T(1,128)}), f32[128,1,1024]{2,1,0:T(1,128)S(1)}, u32[]{:S(2)}, u32[]{:S(2)}) async-start(f32[128,1,1024]{2,1,0:T(1,128)} %reshape.542), calls=%async_computation.2 | async-start | bytes 1048576 | tf_op jit(solution)/shard_map/all_to_all | solution.py:114
  121.5 1.2 copy-start
  152.7 33.1 %copy-start.15 = (f32[2]{0:T(128)}, f32[2]{0:T(128)S(1)}, u32[]{:S(2)}) copy-start(f32[2]{0:T(128)S(1)} %div.6) | copy-start | bytes 28
  152.9 32.9 %copy-start.4 = (f32[2,16,2048]{2,1,0:T(8,128)}, f32[2,16,2048]{2,1,0:T(8,128)S(1)}, u32[]{:S(2)}) copy-start(f32[2,16,2048]{2,1,0:T(8,128)S(1)} %get-tuple-element.10) | copy-start | bytes 786436
where the time goes:
time: 188 us; the launch traced here: 186 us
  blocking collectives  62 us (33%)
  starting transfers between devices  42.9 us (23%)
  waiting for transfers between devices  38 us (20%)
  other arithmetic  20.1 us (11%)
  local copies, waits for them, and re-layouts  13.8 us (7%)
  matrix products  7.17 us (4%)
    psum x6, blocking collectives, over_axes(): return functools.reduce(lax.psum, axes, value)  62 us
    all_to_all x2, starting transfers between devices, exchange_in_pieces(): lax.all_to_all(share, axis, split_axis=0, concat_axis=0, tiled=True)  35.2 us
    all_to_all x2, waiting for transfers between devices, exchange_in_pieces(): lax.all_to_all(share, axis, split_axis=0, concat_axis=0, tiled=True)  19.5 us
    all_to_all x1, waiting for transfers between devices, body(): lax.all_to_all(grid_cols, ROW_SUB, split_axis=1, concat_axis=2, tiled=True)  18.6 us
    unnamed x1, other arithmetic  9.61 us
    all_to_all x1, starting transfers between devices, body(): lax.all_to_all(grid_cols, ROW_SUB, split_axis=1, concat_axis=2, tiled=True)  7.71 us
    unnamed x39, local copies, waits for them, and re-layouts  7.4 us
    dot_general x8, matrix products, contract(): jnp.einsum(form_spec, operand, table_arr, precision=lax.Precision.HIGHEST)  7.17 us
  transfers between devices with their start and end apart: 3, of which 3 were waited for; matrix products, arithmetic and copies ran while one was open for 5% of the time, Pallas kernels for 0%

commit v1 on v0

v1 whole, which is shorter than its diff:
```python
import functools
import math

import jax
import jax.numpy as jnp
import ml_dtypes
import numpy as np
from jax import lax
from jax.experimental import pallas as pl
from jax.experimental.pallas import tpu as pltpu
from jax.sharding import PartitionSpec as P

ROW_SUB = ("row", "sub")
MESH = pl.DeviceIdType.MESH
TINY = 1e-06
LANES = 128
RADIX = 16
F32 = jnp.float32
BF16 = jnp.bfloat16


def roots(left, right, modulus, sign):
    turns = np.mod(np.outer(left, right), modulus)
    return np.exp(sign * 2j * np.pi * turns / modulus)


def real_form(table):
    return np.block([[table.real, -table.imag], [table.imag, table.real]])


def halves(table):
    high = table.astype(ml_dtypes.bfloat16)
    low = (table - high.astype(np.float64)).astype(ml_dtypes.bfloat16)
    return np.stack([high, low])


def tables(rows_dev, grid_len, devices):
    embed = 2 * grid_len
    lane_ids = np.arange(LANES)
    dev_ids = np.arange(devices)
    block = LANES // RADIX
    long_row = real_form(roots(dev_ids, lane_ids, LANES, -1))
    low_ids = np.arange(embed // RADIX)
    long_col = real_form(roots(low_ids, dev_ids, embed // RADIX, -1))
    short = roots(np.arange(RADIX), np.arange(RADIX), RADIX, -1)
    mixed = np.zeros((block, RADIX, RADIX, block), complex)
    for e in range(block):
        mixed[e, :, :, e] = short
    mixed = mixed.reshape(LANES, LANES)
    short_col = real_form(mixed.T).T
    short_back = real_form(np.conj(mixed)).T
    long_back = real_form(np.conj(roots(dev_ids, low_ids, embed // RADIX, -1)))
    half = long_back.shape[1] // 2
    row_back = real_form(np.conj(roots(lane_ids, dev_ids, LANES, -1))).T
    stacked = np.concatenate(
        [long_row, long_col, short_col, short_back, long_back[:, :half], long_back[:, half:], row_back], axis=0
    )
    consts = halves(stacked)
    turn_col = np.tile(roots(low_ids, np.arange(RADIX), embed, -1), (1, block))
    turn_col = np.stack([turn_col.real, turn_col.imag]).astype(np.float32)
    turn_row = np.zeros((2, 2 * RADIX, 2, LANES))
    for ch in range(2):
        for e in range(RADIX):
            turn = roots([2 * e + ch], lane_ids, embed, -1)[0]
            turn_row[ch, e] = [turn.real, turn.imag]
            odd = np.exp(-2j * np.pi * e * ch / (2 * RADIX))
            turn_row[ch, RADIX + e, 0] = odd.real
            turn_row[ch, RADIX + e, 1] = odd.imag
    turn_row = turn_row.reshape(2, 4 * RADIX, LANES).astype(np.float32)
    width = 2 * RADIX
    pick = np.zeros((RADIX, width, 2, 2, RADIX, block))
    for high in range(RADIX):
        for ch in range(2):
            for tile in range(2):
                for e in range(block):
                    pick[high, 2 * (block * tile + e) + ch, ch, tile, high, e] = 1
    pick = pick.reshape(RADIX * width, 4 * LANES).astype(ml_dtypes.bfloat16)
    return consts, turn_col, turn_row, pick


def add(x, y):
    return (x[0] + y[0], x[1] + y[1])


def sub(x, y):
    return (x[0] - y[0], x[1] - y[1])


def times(x, y):
    return (x[0] * y[0] - x[1] * y[1], x[0] * y[1] + x[1] * y[0])


def times_conj(x, y):
    return (x[0] * y[0] + x[1] * y[1], x[1] * y[0] - x[0] * y[1])


def by_root(x, power, sign):
    power %= RADIX
    if power == 0:
        return x
    if power == 4:
        return (x[1], -x[0]) if sign < 0 else (-x[1], x[0])
    if power == 8:
        return (-x[0], -x[1])
    angle = sign * 2.0 * math.pi * power / RADIX
    return times(x, (math.cos(angle), math.sin(angle)))


def four(x, sign):
    even, odd = add(x[0], x[2]), sub(x[0], x[2])
    both, diff = add(x[1], x[3]), sub(x[1], x[3])
    turned = (diff[1], -diff[0]) if sign < 0 else (-diff[1], diff[0])
    return [add(even, both), add(odd, turned), sub(even, both), sub(odd, turned)]


def sixteen(x, sign):
    inner = [four([x[4 * i + j] for i in range(4)], sign) for j in range(4)]
    out = [None] * RADIX
    for first in range(4):
        column = [by_root(inner[j][first], j * first, sign) for j in range(4)]
        for second, value in enumerate(four(column, sign)):
            out[first + 4 * second] = value
    return out


def split(value):
    high = value.astype(BF16)
    return high, (value - high.astype(F32)).astype(BF16)


def dot(left, right, transposed=False):
    dims = (((1,), (1 if transposed else 0,)), ((), ()))
    return lax.dot_general(left, right, dims, preferred_element_type=F32)


def dot3(left, right, transposed=False):
    return (
        dot(left[1], right[0], transposed) + dot(left[0], right[1], transposed) + dot(left[0], right[0], transposed)
    )


def far_first(n_row, n_sub):
    def chips(row, sub_):
        hop = row // 2
        return min(hop, n_row // 2 - hop) + min(sub_, n_sub - sub_)

    offsets = [(i, j) for i in range(n_row) for j in range(n_sub)][1:]
    return sorted(offsets, key=lambda pair: -chips(*pair))


def kernel(
    n_row, n_sub, scale,
    noise_ref, resid_hbm, dir_hbm, spec_hbm, consts_hbm, turn_col_hbm, turn_row_hbm, pick_hbm,
    resid_out, dir_out, step_out,
    resid, direct, spec, consts, turn_col, turn_row, pick,
    out_f, in_f, out_b, in_b, sums, spec_t, image,
    work, tall, left_hi, left_lo, right_hi, right_lo,
    load_sem, send_f, recv_f, send_b, recv_b, send_s, recv_s,
):
    devices = n_row * n_sub
    row, sub_ = lax.axis_index("row"), lax.axis_index("sub")
    me = row * n_sub + sub_
    offsets = far_first(n_row, n_sub)
    wide = 2 * LANES
    low_len = turn_col.shape[1]

    def load(src, dst, slot):
        copy = pltpu.make_async_copy(src, dst, load_sem.at[slot])
        copy.start()
        return copy

    loads = [
        load(dir_hbm, direct, 0),
        load(turn_row_hbm, turn_row, 1),
        load(consts_hbm, consts, 2),
        load(spec_hbm, spec, 3),
        load(pick_hbm, pick, 4),
        load(turn_col_hbm, turn_col, 5),
        load(resid_hbm, resid, 6),
    ]

    def peer(i, j):
        return lax.rem(row + i, n_row), lax.rem(sub_ + j, n_sub)

    barrier = pltpu.get_barrier_semaphore()

    def greet(t, carry):
        other = peer(t // n_sub, lax.rem(t, n_sub))
        pl.semaphore_signal(
            barrier, inc=1, device_id={"row": other[0], "sub": other[1]}, device_id_type=MESH
        )
        return carry

    lax.fori_loop(1, devices, greet, 0)

    def const(index, count=1):
        rows = pl.ds(wide * index, wide * count)
        return consts[0, rows, :], consts[1, rows, :]

    def send_all(src, dst, ch, send_sem, recv_sem):
        part = pl.ds(4 * ch, 4)
        for i, j in offsets:
            to_row, to_sub = peer(i, j)
            pltpu.make_async_remote_copy(
                src.at[to_row * n_sub + to_sub, part],
                dst.at[me, part],
                send_sem.at[ch],
                recv_sem.at[ch],
                device_id={"row": to_row, "sub": to_sub},
                device_id_type=MESH,
            ).start()
        dst[me, part] = src[me, part]

    def wait_all(ref, ch, sem):
        others = ref.at[pl.ds(0, devices - 1), pl.ds(4 * ch, 4)]
        pltpu.make_async_copy(others, others, sem.at[ch]).wait()

    def flat(ref):
        return ref.reshape(devices * 8, LANES)

    def turn(ch, index):
        both = turn_row[ch, pl.ds(2 * index, 2), :]
        return both[0:1], both[1:2]

    loads[0].wait()
    loads[1].wait()
    loads[2].wait()

    def rows_forward(ch, carry):
        for top in range(2):
            lines = pl.ds(8 * top, 8)
            values = []
            for a in range(RADIX):
                lanes = pl.ds(LANES * a, LANES)
                values.append(times((direct[0, lines, lanes], direct[1, lines, lanes]), turn(ch, RADIX + a)))
            for e, value in enumerate(sixteen(values, -1)):
                value = times(value, turn(ch, e))
                for part in range(2):
                    work[pl.ds(RADIX * e + 8 * top, 8), pl.ds(LANES * part, LANES)] = value[part]
        for at in range(0, wide, 32):
            lines = pl.ds(at, 32)
            right_hi[lines, :], right_lo[lines, :] = split(work[lines, :])
        freq = dot3(const(0), (right_hi[pl.ds(0, wide), :], right_lo[pl.ds(0, wide), :]), transposed=True)
        for part in range(2):
            for tile in range(2):
                flat(out_f)[pl.ds(4 * ch + 2 * part + tile, devices, stride=8), :] = freq[
                    devices * part : devices * (part + 1), LANES * tile : LANES * (tile + 1)
                ]

        @pl.when(ch == 0)
        def _():
            pl.semaphore_wait(barrier, devices - 1)

        send_all(out_f, in_f, ch, send_f, recv_f)
        return carry

    lax.fori_loop(0, 2, rows_forward, 0)

    loads[3].wait()
    loads[4].wait()
    loads[5].wait()
    loads[6].wait()
    for at in range(0, low_len, 64):
        parts = [spec[pl.ds(low_len * high + at, 64), :] for high in range(RADIX)]
        joined = jnp.concatenate(parts, axis=1) * scale
        first = joined.astype(BF16)
        rest = joined - first.astype(F32)
        second, third = split(rest)
        spec_t[pl.ds(at, 64), :] = (dot(third, pick[...]) + dot(second, pick[...])) + dot(first, pick[...])

    def columns(ch, carry):
        wait_all(in_f, ch, recv_f)
        for part in range(2):
            for tile in range(2):
                here = (pl.ds(devices * part, devices), pl.ds(LANES * tile, LANES))
                right_hi[here], right_lo[here] = split(
                    flat(in_f)[pl.ds(4 * ch + 2 * part + tile, devices, stride=8), :]
                )
        tall[...] = dot3(const(1, 2), (right_hi[pl.ds(0, wide), :], right_lo[pl.ds(0, wide), :]))
        step = 32
        for tile in range(2):
            lanes = pl.ds(LANES * tile, LANES)
            for at in range(0, low_len, step):
                lines = pl.ds(at, step)
                value = times(
                    (tall[lines, lanes], tall[pl.ds(low_len + at, step), lanes]),
                    (turn_col[0, lines, :], turn_col[1, lines, :]),
                )
                for part in range(2):
                    here = (pl.ds(low_len * tile + at, step), pl.ds(LANES * part, LANES))
                    left_hi[here], left_lo[here] = split(value[part])
        tall[...] = dot3((left_hi[...], left_lo[...]), const(3))
        for tile in range(2):
            for at in range(0, low_len, step):
                weight = spec_t[pl.ds(at, step), pl.ds(pl.multiple_of(wide * ch + LANES * tile, LANES), LANES)]
                for part in range(2):
                    here = (pl.ds(low_len * tile + at, step), pl.ds(LANES * part, LANES))
                    left_hi[here], left_lo[here] = split(tall[here] * weight)
        tall[...] = dot3((left_hi[...], left_lo[...]), const(4))
        for tile in range(2):
            for at in range(0, low_len, step):
                lines = pl.ds(at, step)
                here = pl.ds(low_len * tile + at, step)
                value = times_conj(
                    (tall[here, pl.ds(0, LANES)], tall[here, pl.ds(LANES, LANES)]),
                    (turn_col[0, lines, :], turn_col[1, lines, :]),
                )
                for part in range(2):
                    there = (pl.ds(low_len * part + at, step), pl.ds(LANES * tile, LANES))
                    right_hi[there], right_lo[there] = split(value[part])
        low, high = pl.ds(0, low_len), pl.ds(low_len, low_len)
        grid = dot3(const(5), (right_hi[low, :], right_lo[low, :])) + dot3(
            const(6), (right_hi[high, :], right_lo[high, :])
        )
        for part in range(2):
            for tile in range(2):
                flat(out_b)[pl.ds(4 * ch + 2 * part + tile, devices, stride=8), :] = grid[
                    devices * part : devices * (part + 1), LANES * tile : LANES * (tile + 1)
                ]
        send_all(out_b, in_b, ch, send_b, recv_b)
        return carry

    lax.fori_loop(0, 2, columns, 0)

    noise = noise_ref[0]
    image[...] = noise * direct[...]

    def rows_back(ch, carry):
        wait_all(in_b, ch, recv_b)
        for part in range(2):
            for tile in range(2):
                here = (pl.ds(LANES * tile, LANES), pl.ds(devices * part, devices))
                block = flat(in_b)[pl.ds(4 * ch + 2 * part + tile, devices, stride=8), :]
                left_hi[here], left_lo[here] = split(block.T)
        work[...] = dot3((left_hi[pl.ds(0, wide), :], left_lo[pl.ds(0, wide), :]), const(7))
        for top in range(2):
            values = []
            for e in range(RADIX):
                lines = pl.ds(RADIX * e + 8 * top, 8)
                values.append(
                    times_conj((work[lines, pl.ds(0, LANES)], work[lines, pl.ds(LANES, LANES)]), turn(ch, e))
                )
            lines = pl.ds(8 * top, 8)
            for a, value in enumerate(sixteen(values, 1)):
                value = times_conj(value, turn(ch, RADIX + a))
                lanes = pl.ds(LANES * a, LANES)
                for part in range(2):
                    image[part, lines, lanes] += value[part]
        return carry

    lax.fori_loop(0, 2, rows_back, 0)

    def sum_rows(value):
        return jnp.sum(value, axis=0, keepdims=True)

    lines = []
    for probe in range(2):
        totals = [jnp.zeros((8, LANES), F32) for _ in range(4)]
        for top in range(2):
            for a in range(direct.shape[2] // LANES):
                here = (probe, pl.ds(8 * top, 8), pl.ds(LANES * a, LANES))
                r, d, q = resid[here], direct[here], image[here]
                for index, term in enumerate((r * r, d * q, r * q, q * q)):
                    totals[index] += term
        lines += [sum_rows(total) for total in totals]
    stacked = jnp.sum(jnp.concatenate(lines, axis=0), axis=1, keepdims=True)
    at_row = lax.broadcasted_iota(jnp.int32, (8, LANES), 0)
    at_lane = lax.broadcasted_iota(jnp.int32, (8, LANES), 1)
    mine = sum_rows(jnp.where(at_row == at_lane, stacked, 0.0))
    sums[me] = mine

    def tell(t, carry):
        to_row, to_sub = peer(t // n_sub, lax.rem(t, n_sub))
        pltpu.make_async_remote_copy(
            sums.at[me], sums.at[me], send_s, recv_s,
            device_id={"row": to_row, "sub": to_sub}, device_id_type=MESH,
        ).start()
        return carry

    lax.fori_loop(1, devices, tell, 0)
    for ch in range(2):
        wait_all(out_f, ch, send_f)
        wait_all(out_b, ch, send_b)
    others = sums.at[pl.ds(0, devices - 1)]
    pltpu.make_async_copy(others, others, send_s).wait()
    pltpu.make_async_copy(others, others, recv_s).wait()
    total = jnp.sum(sums[...], axis=0)

    sizes = []
    for probe in range(2):
        old_norm, curvature, cross, square = (total[:, 4 * probe + i : 4 * probe + i + 1] for i in range(4))
        size = old_norm / curvature
        new_norm = old_norm - 2.0 * (size * cross) + size * (size * square)
        ratio = new_norm / (old_norm + TINY)
        sizes.append(size)
        for a in range(direct.shape[2] // LANES):
            here = (probe, slice(None), pl.ds(LANES * a, LANES))
            value = resid[here] - size * image[here]
            resid_out[here] = value
            dir_out[here] = value + ratio * direct[here]
    lane = lax.broadcasted_iota(jnp.int32, (1, LANES), 1)
    step_out[...] = jnp.where(lane == 0, sizes[0], sizes[1])


def body(n_row, n_sub, residual_in, direction, spectrum, noise_var):
    probes, rows_dev, grid_len = direction.shape
    devices = n_row * n_sub
    embed = 2 * grid_len
    consts, turn_col, turn_row, pick = tables(rows_dev, grid_len, devices)
    low_len = embed // RADIX
    wide = 2 * LANES
    slots = (devices, 8, LANES)
    vmem = pltpu.VMEM
    sems = pltpu.SemaphoreType.DMA
    block = (probes, rows_dev, grid_len)
    any_spec = pl.BlockSpec(memory_space=pl.ANY)
    vmem_spec = pl.BlockSpec(memory_space=pltpu.VMEM)
    resid, direct, step = pl.pallas_call(
        functools.partial(kernel, n_row, n_sub, 1.0 / (embed * embed)),
        out_shape=(
            jax.ShapeDtypeStruct(block, F32),
            jax.ShapeDtypeStruct(block, F32),
            jax.ShapeDtypeStruct((1, LANES), F32),
        ),
        in_specs=[pl.BlockSpec(memory_space=pltpu.SMEM)] + [any_spec] * 7,
        out_specs=(vmem_spec,) * 3,
        scratch_shapes=[
            vmem(block, F32), vmem(block, F32), vmem(spectrum.shape, F32),
            vmem(consts.shape, BF16), vmem(turn_col.shape, F32), vmem(turn_row.shape, F32), vmem(pick.shape, BF16),
            vmem(slots, F32), vmem(slots, F32), vmem(slots, F32), vmem(slots, F32),
            vmem((devices, 1, LANES), F32), vmem((low_len, 4 * LANES), F32), vmem(block, F32),
            vmem((wide, wide), F32), vmem((2 * low_len, wide), F32),
            vmem((2 * low_len, wide), BF16), vmem((2 * low_len, wide), BF16),
            vmem((2 * low_len, wide), BF16), vmem((2 * low_len, wide), BF16),
            sems((7,)), sems((2,)), sems((2,)), sems((2,)), sems((2,)), sems, sems,
        ],
        compiler_params=pltpu.CompilerParams(collective_id=0, has_side_effects=True),
        name="cg_step",
    )(noise_var, residual_in, direction, spectrum, *(jnp.asarray(t) for t in (consts, turn_col, turn_row, pick)))
    return resid, direct, step[0, :probes]


def solution(mesh):
    in_specs = (P("grp", ROW_SUB, None), P("grp", ROW_SUB, None), P("grp", ROW_SUB), P("grp"))
    out_specs = (P("grp", ROW_SUB, None), P("grp", ROW_SUB, None), P("grp"))
    return jax.shard_map(
        functools.partial(body, mesh.shape["row"], mesh.shape["sub"]),
        mesh=mesh, in_specs=in_specs, out_specs=out_specs, check_vma=False,
    )
```

time: 188 us -> 75.1 us (0.40); the launches traced: 186 us -> 74.9 us
  Pallas kernels: 0 us -> 66.1 us
  blocking collectives: 62 us -> 0 us
  starting transfers between devices: 42.9 us -> 0 us
  waiting for transfers between devices: 38 us -> 0 us
  other arithmetic: 20.1 us -> 0 us
  matrix products: 7.17 us -> 0 us
  local copies, waits for them, and re-layouts: 13.8 us -> 7.52 us
    pallas_call x0 -> x1, Pallas kernels: none -> 66.1 us  [body(): pl.pallas_call(functools.partial(kernel, n_row, n_sub, 1.0 / (embed * emb...]
    psum x6 -> x0, blocking collectives: 62 us -> none  [over_axes(): return functools.reduce(lax.psum, axes, value)]
    all_to_all x3 -> x0, starting transfers between devices: 42.9 us -> none  [the longest x2 35.2 us: exchange_in_pieces(): lax.all_to_all(share, axis, split_axis=0, concat_axis=0, tiled=True)]
    all_to_all x3 -> x0, waiting for transfers between devices: 38 us -> none  [the longest x2 19.5 us: exchange_in_pieces(): lax.all_to_all(share, axis, split_axis=0, concat_axis=0, tiled=True)]
    unnamed x1 -> x0, other arithmetic: 9.61 us -> none
    dot_general x8 -> x0, matrix products: 7.17 us -> none  [contract(): jnp.einsum(form_spec, operand, table_arr, precision=lax.Precision.HIGHEST)]
    all_to_all x3 -> x0, other arithmetic: 4.4 us -> none  [the longest x2 2.52 us: exchange_in_pieces(): lax.all_to_all(share, axis, split_axis=0, concat_axis=0, tiled=True)]
    mul x2 -> x0, local copies, waits for them, and re-layouts: 2.14 us -> none  [body(): spectra = spectra * weights[None, :, :, :, None, :]]
  transfers between devices with their start and end apart: 3 -> 0, of which waited for: 3 -> 0; matrix products, arithmetic and copies ran while one was open for 5% -> 0% of each run, Pallas kernels for 0% -> 0%
where the time goes in v1:
time: 75.1 us; the launch traced here: 74.9 us
  Pallas kernels  66.1 us (88%)
  local copies, waits for them, and re-layouts  7.52 us (10%)
  between operations  1.29 us (2%)
    pallas_call x1, Pallas kernels, body(): pl.pallas_call(functools.partial(kernel, n_row, n_sub, 1.0 / (embed * emb...  66.1 us
    unnamed x3, local copies, waits for them, and re-layouts  6.34 us

profile of v1, /device:TPU:513, one launch (start us, length us, event | category | flops | bytes accessed | tf_op | source)
XLA Modules:
  0.0 74.9 jit_solution(12843687474535775036)
XLA Ops:
  1.3 3.0 %copy.11.spec_hbm = f32[4096,32]{1,0:T(8,128)} copy(f32[4096,32]{0,1:T(8,128)} %param.10) | data formatting | bytes 1048576 | tf_op args[2]
  4.3 66.1 %cg_step.1 = (f32[2,16,2048]{2,1,0:T(8,128)}, f32[2,16,2048]{2,1,0:T(8,128)}, f32[1,128]{1,0:T(1,128)}) custom-call(f32[1]{0:T(128)S(6)} %copy.14.noise_ref, f32[2,16,2048]{2,1,0:T(8,128)} %resid_hbm.1, f32[2,16,2048]{2,1,0:T(8,128)} %dir_hbm.1, f32[4096,32]{1,0:T(8,128)} %copy.11.spec_hbm, bf16[2,2048,256]{2,1,0:T(8,128)(2,1)} %constant.8.clone.consts_hbm, ...), custom_call_target="tpu_custom_call" | custom-call | tf_op jit(solution)/shard_map/cg_step/pallas_call | solution.py:418
  70.3 1.2 %slice_bitcast_fusion = f32[2]{0:T(128)} fusion(f32[1,128]{1,0:T(1,128)} %get-tuple-element.8), kind=kLoop, calls=%fused_computation | loop fusion | bytes 16 | tf_op jit(solution)/shard_map/squeeze | solution.py:440
  71.5 1.7 %copy.15 = f32[2,16,2048]{2,1,0:T(8,128)} copy(f32[2,16,2048]{2,1,0:T(8,128)} %get-tuple-element.12) | data formatting | bytes 524288
  73.2 1.7 %copy.16 = f32[2,16,2048]{2,1,0:T(8,128)} copy(f32[2,16,2048]{2,1,0:T(8,128)} %get-tuple-element.13) | data formatting | bytes 524288

commit v2 on v1

--- a/solution.py
+++ b/solution.py
@@ -67,15 +67,7 @@
             turn_row[ch, RADIX + e, 0] = odd.real
             turn_row[ch, RADIX + e, 1] = odd.imag
     turn_row = turn_row.reshape(2, 4 * RADIX, LANES).astype(np.float32)
-    width = 2 * RADIX
-    pick = np.zeros((RADIX, width, 2, 2, RADIX, block))
-    for high in range(RADIX):
-        for ch in range(2):
-            for tile in range(2):
-                for e in range(block):
-                    pick[high, 2 * (block * tile + e) + ch, ch, tile, high, e] = 1
-    pick = pick.reshape(RADIX * width, 4 * LANES).astype(ml_dtypes.bfloat16)
-    return consts, turn_col, turn_row, pick
+    return consts, turn_col, turn_row
 
 
 def add(x, y):
@@ -148,14 +140,18 @@
     return sorted(offsets, key=lambda pair: -chips(*pair))
 
 
+def outward(count):
+    return [count // 2 + (1 - 2 * (t % 2)) * ((t + 1) // 2) for t in range(count)]
+
+
 def kernel(
     n_row, n_sub, scale,
-    noise_ref, resid_hbm, dir_hbm, spec_hbm, consts_hbm, turn_col_hbm, turn_row_hbm, pick_hbm,
-    resid_out, dir_out, step_out,
-    resid, direct, spec, consts, turn_col, turn_row, pick,
+    noise_ref, resid_hbm, dir_hbm, spec_hbm, consts_hbm, turn_col_hbm, turn_row_hbm,
+    image_out, total_out,
+    resid, direct, spec, consts, turn_col, turn_row,
     out_f, in_f, out_b, in_b, sums, spec_t, image,
     work, tall, left_hi, left_lo, right_hi, right_lo,
-    load_sem, send_f, recv_f, send_b, recv_b, send_s, recv_s,
+    load_sem, store_sem, send_f, recv_f, send_b, recv_b, send_s, recv_s,
 ):
     devices = n_row * n_sub
     row, sub_ = lax.axis_index("row"), lax.axis_index("sub")
@@ -169,29 +165,40 @@
         copy.start()
         return copy
 
+    def wrap(value, count):
+        return jnp.where(value >= count, value - count, value)
+
+    def peer(i, j):
+        return wrap(row + i, n_row), wrap(sub_ + j, n_sub)
+
+    subs = [wrap(sub_ + j, n_sub) for j in outward(n_sub)]
+
+    def each_peer(act):
+        def one_row(t, carry):
+            half = n_row // 2
+            to_row = wrap(row + half + (1 - 2 * (t % 2)) * ((t + 1) // 2), n_row)
+            for to_sub in subs:
+                act(to_row, to_sub)
+            return carry
+
+        lax.fori_loop(0, n_row - 1, one_row, 0)
+        for to_sub in subs[:-1]:
+            act(row, to_sub)
+
+    barrier = pltpu.get_barrier_semaphore()
+
+    def greet(to_row, to_sub):
+        pl.semaphore_signal(barrier, inc=1, device_id={"row": to_row, "sub": to_sub}, device_id_type=MESH)
+
+    each_peer(greet)
     loads = [
         load(dir_hbm, direct, 0),
         load(turn_row_hbm, turn_row, 1),
         load(consts_hbm, consts, 2),
-        load(spec_hbm, spec, 3),
-        load(pick_hbm, pick, 4),
-        load(turn_col_hbm, turn_col, 5),
-        load(resid_hbm, resid, 6),
+        load(turn_col_hbm, turn_col, 3),
+        load(resid_hbm, resid, 4),
     ]
-
-    def peer(i, j):
-        return lax.rem(row + i, n_row), lax.rem(sub_ + j, n_sub)
-
-    barrier = pltpu.get_barrier_semaphore()
-
-    def greet(t, carry):
-        other = peer(t // n_sub, lax.rem(t, n_sub))
-        pl.semaphore_signal(
-            barrier, inc=1, device_id={"row": other[0], "sub": other[1]}, device_id_type=MESH
-        )
-        return carry
-
-    lax.fori_loop(1, devices, greet, 0)
+    loads += [load(spec_hbm.at[:, pl.ds(LANES * t, LANES)], spec.at[t], 5) for t in range(spec.shape[0])]
 
     def const(index, count=1):
         rows = pl.ds(wide * index, wide * count)
@@ -256,17 +263,20 @@
 
     lax.fori_loop(0, 2, rows_forward, 0)
 
-    loads[3].wait()
-    loads[4].wait()
-    loads[5].wait()
-    loads[6].wait()
-    for at in range(0, low_len, 64):
-        parts = [spec[pl.ds(low_len * high + at, 64), :] for high in range(RADIX)]
-        joined = jnp.concatenate(parts, axis=1) * scale
-        first = joined.astype(BF16)
-        rest = joined - first.astype(F32)
-        second, third = split(rest)
-        spec_t[pl.ds(at, 64), :] = (dot(third, pick[...]) + dot(second, pick[...])) + dot(first, pick[...])
+    for copy in loads[3:5]:
+        copy.wait()
+    pltpu.make_async_copy(spec, spec, load_sem.at[5]).wait()
+    spec_rows = spec.reshape(spec.shape[0] * spec.shape[1], LANES)
+    for ch in range(2):
+        for tile in range(2):
+            for top in range(low_len // LANES):
+                parts = []
+                for high in range(RADIX):
+                    at = spec.shape[1] * ((low_len // LANES) * high + top) + RADIX * tile + ch
+                    parts.append(spec_rows[pl.ds(at, 8, stride=2), :])
+                spec_t[pl.ds(LANES * top, LANES), pl.ds(wide * ch + LANES * tile, LANES)] = (
+                    jnp.concatenate(parts, axis=0).T * scale
+                )
 
     def columns(ch, carry):
         wait_all(in_f, ch, recv_f)
@@ -349,6 +359,8 @@
         return carry
 
     lax.fori_loop(0, 2, rows_back, 0)
+    leave = pltpu.make_async_copy(image, image_out, store_sem)
+    leave.start()
 
     def sum_rows(value):
         return jnp.sum(value, axis=0, keepdims=True)
@@ -369,75 +381,81 @@
     mine = sum_rows(jnp.where(at_row == at_lane, stacked, 0.0))
     sums[me] = mine
 
-    def tell(t, carry):
-        to_row, to_sub = peer(t // n_sub, lax.rem(t, n_sub))
+    def tell(to_row, to_sub):
         pltpu.make_async_remote_copy(
             sums.at[me], sums.at[me], send_s, recv_s,
             device_id={"row": to_row, "sub": to_sub}, device_id_type=MESH,
         ).start()
-        return carry
-
-    lax.fori_loop(1, devices, tell, 0)
+
+    each_peer(tell)
     for ch in range(2):
         wait_all(out_f, ch, send_f)
         wait_all(out_b, ch, send_b)
     others = sums.at[pl.ds(0, devices - 1)]
     pltpu.make_async_copy(others, others, send_s).wait()
     pltpu.make_async_copy(others, others, recv_s).wait()
-    total = jnp.sum(sums[...], axis=0)
-
-    sizes = []
+    total_out[...] = jnp.sum(sums[...], axis=0)
+    leave.wait()
+
+
+def finish(total_ref, resid, direct, image, resid_out, dir_out, step_out):
+    total = total_ref[...]
     for probe in range(2):
         old_norm, curvature, cross, square = (total[:, 4 * probe + i : 4 * probe + i + 1] for i in range(4))
         size = old_norm / curvature
         new_norm = old_norm - 2.0 * (size * cross) + size * (size * square)
         ratio = new_norm / (old_norm + TINY)
-        sizes.append(size)
+        step_out[probe] = size[0, 0]
         for a in range(direct.shape[2] // LANES):
             here = (probe, slice(None), pl.ds(LANES * a, LANES))
             value = resid[here] - size * image[here]
             resid_out[here] = value
             dir_out[here] = value + ratio * direct[here]
-    lane = lax.broadcasted_iota(jnp.int32, (1, LANES), 1)
-    step_out[...] = jnp.where(lane == 0, sizes[0], sizes[1])
 
 
 def body(n_row, n_sub, residual_in, direction, spectrum, noise_var):
     probes, rows_dev, grid_len = direction.shape
     devices = n_row * n_sub
     embed = 2 * grid_len
-    consts, turn_col, turn_row, pick = tables(rows_dev, grid_len, devices)
+    consts, turn_col, turn_row = tables(rows_dev, grid_len, devices)
     low_len = embed // RADIX
     wide = 2 * LANES
     slots = (devices, 8, LANES)
     vmem = pltpu.VMEM
     sems = pltpu.SemaphoreType.DMA
     block = (probes, rows_dev, grid_len)
-    any_spec = pl.BlockSpec(memory_space=pl.ANY)
+    hbm_spec = pl.BlockSpec(memory_space=pltpu.HBM)
     vmem_spec = pl.BlockSpec(memory_space=pltpu.VMEM)
-    resid, direct, step = pl.pallas_call(
+    smem_spec = pl.BlockSpec(memory_space=pltpu.SMEM)
+    image, total = pl.pallas_call(
         functools.partial(kernel, n_row, n_sub, 1.0 / (embed * embed)),
-        out_shape=(
-            jax.ShapeDtypeStruct(block, F32),
-            jax.ShapeDtypeStruct(block, F32),
-            jax.ShapeDtypeStruct((1, LANES), F32),
-        ),
-        in_specs=[pl.BlockSpec(memory_space=pltpu.SMEM)] + [any_spec] * 7,
-        out_specs=(vmem_spec,) * 3,
+        out_shape=(jax.ShapeDtypeStruct(block, F32), jax.ShapeDtypeStruct((1, LANES), F32)),
+        in_specs=[smem_spec] + [hbm_spec] * 6,
+        out_specs=(hbm_spec, vmem_spec),
         scratch_shapes=[
-            vmem(block, F32), vmem(block, F32), vmem(spectrum.shape, F32),
-            vmem(consts.shape, BF16), vmem(turn_col.shape, F32), vmem(turn_row.shape, F32), vmem(pick.shape, BF16),
+            vmem(block, F32), vmem(block, F32), vmem((embed // LANES, spectrum.shape[1], LANES), F32),
+            vmem(consts.shape, BF16), vmem(turn_col.shape, F32), vmem(turn_row.shape, F32),
             vmem(slots, F32), vmem(slots, F32), vmem(slots, F32), vmem(slots, F32),
             vmem((devices, 1, LANES), F32), vmem((low_len, 4 * LANES), F32), vmem(block, F32),
             vmem((wide, wide), F32), vmem((2 * low_len, wide), F32),
             vmem((2 * low_len, wide), BF16), vmem((2 * low_len, wide), BF16),
             vmem((2 * low_len, wide), BF16), vmem((2 * low_len, wide), BF16),
-            sems((7,)), sems((2,)), sems((2,)), sems((2,)), sems((2,)), sems, sems,
+            sems((6,)), sems, sems((2,)), sems((2,)), sems((2,)), sems((2,)), sems, sems,
         ],
         compiler_params=pltpu.CompilerParams(collective_id=0, has_side_effects=True),
         name="cg_step",
-    )(noise_var, residual_in, direction, spectrum, *(jnp.asarray(t) for t in (consts, turn_col, turn_row, pick)))
-    return resid, direct, step[0, :probes]
+    )(noise_var, residual_in, direction, spectrum.T, *(jnp.asarray(t) for t in (consts, turn_col, turn_row)))
+    return pl.pallas_call(
+        finish,
+        out_shape=(
+            jax.ShapeDtypeStruct(block, F32),
+            jax.ShapeDtypeStruct(block, F32),
+            jax.ShapeDtypeStruct((probes,), F32),
+        ),
+        in_specs=[vmem_spec] * 4,
+        out_specs=(vmem_spec, vmem_spec, smem_spec),
+        name="finish",
+    )(total, residual_in, direction, image)
 
 
 def solution(mesh):

time: 75.1 us -> 67.2 us (0.89)
  local copies, waits for them, and re-layouts: 7.52 us -> 0 us
    unnamed x3 -> x0, local copies, waits for them, and re-layouts: 6.34 us -> none
    pallas_call x1, Pallas kernels: 66.1 us -> 63.7 us  [body(): pl.pallas_call(functools.partial(kernel, n_row, n_sub, 1.0 / (embed * emb...]
    pallas_call x0 -> x1, Pallas kernels: none -> 2.1 us  [body(): pl.pallas_call(finish, out_shape=(jax.ShapeDtypeStruct(block, F32), jax.S...]
    squeeze x1 -> x0, local copies, waits for them, and re-layouts: 1.18 us -> none  [body(): return (resid, direct, step[0, :probes])]
where the time goes in v2:
time: 67.2 us; the launch traced here: 67.1 us
  Pallas kernels  65.8 us (98%)
  between operations  1.28 us (2%)
    pallas_call x1, Pallas kernels, body(): pl.pallas_call(functools.partial(kernel, n_row, n_sub, 1.0 / (embed * emb...  63.7 us
    pallas_call x1, Pallas kernels, body(): pl.pallas_call(finish, out_shape=(jax.ShapeDtypeStruct(block, F32), jax.S...  2.1 us

profile of v2, /device:TPU:513, one launch (start us, length us, event | category | flops | bytes accessed | tf_op | source)
XLA Modules:
  0.0 67.1 jit_solution(3655141224083333245)
XLA Ops:
  1.3 63.7 %cg_step.1 = (f32[2,16,2048]{2,1,0:T(8,128)}, f32[1,128]{1,0:T(1,128)}) custom-call(f32[1]{0:T(128)S(6)} %copy.10.noise_ref, f32[2,16,2048]{2,1,0:T(8,128)} %resid.1, f32[2,16,2048]{2,1,0:T(8,128)} %direct.1, f32[32,4096]{1,0:T(8,128)} %bitcast.1, bf16[2,2048,256]{2,1,0:T(8,128)(2,1)} %constant.6.clone.consts_hbm, ...), custom_call_target="tpu_custom_call" | custom-call | tf_op jit(solution)/shard_map/cg_step/pallas_call | solution.py:430
  65.0 2.1 %finish.1 = (f32[2,16,2048]{2,1,0:T(8,128)}, f32[2,16,2048]{2,1,0:T(8,128)}, f32[2]{0:T(128)}) custom-call(f32[1,128]{1,0:T(1,128)} %get-tuple-element.5.total_ref, f32[2,16,2048]{2,1,0:T(8,128)} %resid.1, f32[2,16,2048]{2,1,0:T(8,128)} %direct.1, f32[2,16,2048]{2,1,0:T(8,128)} %get-tuple-element.6.image), custom_call_target="tpu_custom_call" | custom-call | tf_op jit(solution)/shard_map/finish/pallas_call | solution.py:448

commit v3 on v2

--- a/solution.py
+++ b/solution.py
@@ -151,7 +151,7 @@
     resid, direct, spec, consts, turn_col, turn_row,
     out_f, in_f, out_b, in_b, sums, spec_t, image,
     work, tall, left_hi, left_lo, right_hi, right_lo,
-    load_sem, store_sem, send_f, recv_f, send_b, recv_b, send_s, recv_s,
+    load_sem, store_sem, send_f, recv_f, send_b, recv_b, send_s, recv_s, here_sem,
 ):
     devices = n_row * n_sub
     row, sub_ = lax.axis_index("row"), lax.axis_index("sub")
@@ -190,7 +190,13 @@
     def greet(to_row, to_sub):
         pl.semaphore_signal(barrier, inc=1, device_id={"row": to_row, "sub": to_sub}, device_id_type=MESH)
 
-    each_peer(greet)
+    def announce(to_row, to_sub):
+        pl.semaphore_signal(here_sem, inc=1, device_id={"row": to_row, "sub": to_sub}, device_id_type=MESH)
+
+    @pl.when(me != 0)
+    def _():
+        each_peer(greet)
+
     loads = [
         load(dir_hbm, direct, 0),
         load(turn_row_hbm, turn_row, 1),
@@ -204,18 +210,26 @@
         rows = pl.ds(wide * index, wide * count)
         return consts[0, rows, :], consts[1, rows, :]
 
-    def send_all(src, dst, ch, send_sem, recv_sem):
+    def send(src, dst, ch, send_sem, recv_sem, to_row, to_sub):
         part = pl.ds(4 * ch, 4)
+        pltpu.make_async_remote_copy(
+            src.at[to_row * n_sub + to_sub, part],
+            dst.at[me, part],
+            send_sem.at[ch],
+            recv_sem.at[ch],
+            device_id={"row": to_row, "sub": to_sub},
+            device_id_type=MESH,
+        ).start()
+
+    def send_all(src, dst, ch, send_sem, recv_sem, all_here):
         for i, j in offsets:
             to_row, to_sub = peer(i, j)
-            pltpu.make_async_remote_copy(
-                src.at[to_row * n_sub + to_sub, part],
-                dst.at[me, part],
-                send_sem.at[ch],
-                recv_sem.at[ch],
-                device_id={"row": to_row, "sub": to_sub},
-                device_id_type=MESH,
-            ).start()
+            go = functools.partial(send, src, dst, ch, send_sem, recv_sem, to_row, to_sub)
+            if all_here:
+                go()
+            else:
+                pl.when(to_row + to_sub != 0)(go)
+        part = pl.ds(4 * ch, 4)
         dst[me, part] = src[me, part]
 
     def wait_all(ref, ch, sem):
@@ -256,9 +270,13 @@
 
         @pl.when(ch == 0)
         def _():
-            pl.semaphore_wait(barrier, devices - 1)
-
-        send_all(out_f, in_f, ch, send_f, recv_f)
+            pl.semaphore_wait(barrier, jnp.where(me == 0, devices - 1, devices - 2))
+
+            @pl.when(me == 0)
+            def _():
+                each_peer(announce)
+
+        send_all(out_f, in_f, ch, send_f, recv_f, False)
         return carry
 
     lax.fori_loop(0, 2, rows_forward, 0)
@@ -277,6 +295,12 @@
                 spec_t[pl.ds(LANES * top, LANES), pl.ds(wide * ch + LANES * tile, LANES)] = (
                     jnp.concatenate(parts, axis=0).T * scale
                 )
+
+    @pl.when(me != 0)
+    def _():
+        pl.semaphore_wait(here_sem, 1)
+        for ch in range(2):
+            send(out_f, in_f, ch, send_f, recv_f, 0, 0)
 
     def columns(ch, carry):
         wait_all(in_f, ch, recv_f)
@@ -327,7 +351,7 @@
                 flat(out_b)[pl.ds(4 * ch + 2 * part + tile, devices, stride=8), :] = grid[
                     devices * part : devices * (part + 1), LANES * tile : LANES * (tile + 1)
                 ]
-        send_all(out_b, in_b, ch, send_b, recv_b)
+        send_all(out_b, in_b, ch, send_b, recv_b, True)
         return carry
 
     lax.fori_loop(0, 2, columns, 0)
@@ -440,7 +464,7 @@
             vmem((wide, wide), F32), vmem((2 * low_len, wide), F32),
             vmem((2 * low_len, wide), BF16), vmem((2 * low_len, wide), BF16),
             vmem((2 * low_len, wide), BF16), vmem((2 * low_len, wide), BF16),
-            sems((6,)), sems, sems((2,)), sems((2,)), sems((2,)), sems((2,)), sems, sems,
+            sems((6,)), sems, sems((2,)), sems((2,)), sems((2,)), sems((2,)), sems, sems, pltpu.SemaphoreType.REGULAR,
         ],
         compiler_params=pltpu.CompilerParams(collective_id=0, has_side_effects=True),
         name="cg_step",

time: 67.2 us -> 63.4 us (0.943)
  Pallas kernels: 65.8 us -> 62 us
    pallas_call x1, Pallas kernels: 63.7 us -> 59.9 us  [body(): pl.pallas_call(functools.partial(kernel, n_row, n_sub, 1.0 / (embed * emb...]
where the time goes in v3:
time: 63.4 us; the launch traced here: 63.3 us
  Pallas kernels  62 us (98%)
  between operations  1.28 us (2%)
    pallas_call x1, Pallas kernels, body(): pl.pallas_call(functools.partial(kernel, n_row, n_sub, 1.0 / (embed * emb...  59.9 us
    pallas_call x1, Pallas kernels, body(): pl.pallas_call(finish, out_shape=(jax.ShapeDtypeStruct(block, F32), jax.S...  2.1 us

profile of v3, /device:TPU:513, one launch (start us, length us, event | category | flops | bytes accessed | tf_op | source)
XLA Modules:
  0.0 63.3 jit_solution(1669996693743723639)
XLA Ops:
  1.3 59.9 %cg_step.1 = (f32[2,16,2048]{2,1,0:T(8,128)}, f32[1,128]{1,0:T(1,128)}) custom-call(f32[1]{0:T(128)S(6)} %copy.10.noise_ref, f32[2,16,2048]{2,1,0:T(8,128)} %resid.1, f32[2,16,2048]{2,1,0:T(8,128)} %direct.1, f32[32,4096]{1,0:T(8,128)} %bitcast.1, bf16[2,2048,256]{2,1,0:T(8,128)(2,1)} %constant.6.clone.consts_hbm, ...), custom_call_target="tpu_custom_call" | custom-call | tf_op jit(solution)/shard_map/cg_step/pallas_call | solution.py:454
  61.2 2.1 %finish.1 = (f32[2,16,2048]{2,1,0:T(8,128)}, f32[2,16,2048]{2,1,0:T(8,128)}, f32[2]{0:T(128)}) custom-call(f32[1,128]{1,0:T(1,128)} %get-tuple-element.5.total_ref, f32[2,16,2048]{2,1,0:T(8,128)} %resid.1, f32[2,16,2048]{2,1,0:T(8,128)} %direct.1, f32[2,16,2048]{2,1,0:T(8,128)} %get-tuple-element.6.image), custom_call_target="tpu_custom_call" | custom-call | tf_op jit(solution)/shard_map/finish/pallas_call | solution.py:472

commit v4 on v3

--- a/solution.py
+++ b/solution.py
@@ -13,6 +13,7 @@
 ROW_SUB = ("row", "sub")
 MESH = pl.DeviceIdType.MESH
 TINY = 1e-06
+VMEM_LIMIT = 56 << 20
 LANES = 128
 RADIX = 16
 F32 = jnp.float32
@@ -131,15 +132,6 @@
     )
 
 
-def far_first(n_row, n_sub):
-    def chips(row, sub_):
-        hop = row // 2
-        return min(hop, n_row // 2 - hop) + min(sub_, n_sub - sub_)
-
-    offsets = [(i, j) for i in range(n_row) for j in range(n_sub)][1:]
-    return sorted(offsets, key=lambda pair: -chips(*pair))
-
-
 def outward(count):
     return [count // 2 + (1 - 2 * (t % 2)) * ((t + 1) // 2) for t in range(count)]
 
@@ -156,7 +148,6 @@
     devices = n_row * n_sub
     row, sub_ = lax.axis_index("row"), lax.axis_index("sub")
     me = row * n_sub + sub_
-    offsets = far_first(n_row, n_sub)
     wide = 2 * LANES
     low_len = turn_col.shape[1]
 
@@ -168,39 +159,48 @@
     def wrap(value, count):
         return jnp.where(value >= count, value - count, value)
 
-    def peer(i, j):
-        return wrap(row + i, n_row), wrap(sub_ + j, n_sub)
-
-    subs = [wrap(sub_ + j, n_sub) for j in outward(n_sub)]
+    rows = [wrap(row + i, n_row) for i in outward(n_row)]
+
+    def mates(act):
+        for to_row in rows[:-1]:
+            act(to_row, sub_)
+
+    def other_subs(act, wanted):
+        def one_sub(t, carry):
+            to_sub = wrap(sub_ + n_sub // 2 + (1 - 2 * (t % 2)) * ((t + 1) // 2), n_sub)
+
+            @pl.when(wanted(to_sub))
+            def _():
+                for to_row in rows:
+                    act(to_row, to_sub)
+
+            return carry
+
+        lax.fori_loop(0, n_sub - 1, one_sub, 0)
 
     def each_peer(act):
-        def one_row(t, carry):
-            half = n_row // 2
-            to_row = wrap(row + half + (1 - 2 * (t % 2)) * ((t + 1) // 2), n_row)
-            for to_sub in subs:
-                act(to_row, to_sub)
-            return carry
-
-        lax.fori_loop(0, n_row - 1, one_row, 0)
-        for to_sub in subs[:-1]:
-            act(row, to_sub)
-
+        other_subs(act, lambda to_sub: to_sub >= 0)
+        mates(act)
+
+    late = me == 0
+    level = jnp.where(late, n_sub, sub_)
+
+    loads = [load(dir_hbm, direct, 0), load(turn_row_hbm, turn_row, 1), load(consts_hbm, consts, 2)]
     barrier = pltpu.get_barrier_semaphore()
 
     def greet(to_row, to_sub):
         pl.semaphore_signal(barrier, inc=1, device_id={"row": to_row, "sub": to_sub}, device_id_type=MESH)
 
     def announce(to_row, to_sub):
-        pl.semaphore_signal(here_sem, inc=1, device_id={"row": to_row, "sub": to_sub}, device_id_type=MESH)
-
-    @pl.when(me != 0)
+        pl.semaphore_signal(here_sem.at[level], inc=1, device_id={"row": to_row, "sub": to_sub}, device_id_type=MESH)
+
+    @pl.when(jnp.logical_not(late))
     def _():
-        each_peer(greet)
-
-    loads = [
-        load(dir_hbm, direct, 0),
-        load(turn_row_hbm, turn_row, 1),
-        load(consts_hbm, consts, 2),
+        mates(greet)
+        other_subs(greet, lambda to_sub: to_sub > sub_)
+        pl.when(sub_ != 0)(lambda: greet(0, 0))
+
+    loads += [
         load(turn_col_hbm, turn_col, 3),
         load(resid_hbm, resid, 4),
     ]
@@ -221,14 +221,7 @@
             device_id_type=MESH,
         ).start()
 
-    def send_all(src, dst, ch, send_sem, recv_sem, all_here):
-        for i, j in offsets:
-            to_row, to_sub = peer(i, j)
-            go = functools.partial(send, src, dst, ch, send_sem, recv_sem, to_row, to_sub)
-            if all_here:
-                go()
-            else:
-                pl.when(to_row + to_sub != 0)(go)
+    def keep_own(src, dst, ch):
         part = pl.ds(4 * ch, 4)
         dst[me, part] = src[me, part]
 
@@ -270,13 +263,22 @@
 
         @pl.when(ch == 0)
         def _():
-            pl.semaphore_wait(barrier, jnp.where(me == 0, devices - 1, devices - 2))
-
-            @pl.when(me == 0)
+            pl.semaphore_wait(barrier, jnp.where(late, devices - 1, n_row * (sub_ + 1) - 2))
+            pl.when(late)(lambda: each_peer(announce))
+
+            @pl.when(jnp.logical_not(late))
             def _():
-                each_peer(announce)
-
-        send_all(out_f, in_f, ch, send_f, recv_f, False)
+                for to_sub in range(n_sub):
+                    pl.when((to_sub < sub_) & (row + to_sub != 0))(functools.partial(announce, row, to_sub))
+
+        def go(to_row, to_sub):
+            pl.when(to_row + to_sub != 0)(
+                functools.partial(send, out_f, in_f, ch, send_f, recv_f, to_row, to_sub)
+            )
+
+        other_subs(go, lambda to_sub: to_sub <= level)
+        mates(go)
+        keep_own(out_f, in_f, ch)
         return carry
 
     lax.fori_loop(0, 2, rows_forward, 0)
@@ -296,9 +298,21 @@
                     jnp.concatenate(parts, axis=0).T * scale
                 )
 
-    @pl.when(me != 0)
+    def later_class(to_sub, carry):
+        @pl.when(to_sub > level)
+        def _():
+            pl.semaphore_wait(here_sem.at[to_sub], 1)
+            for ch in range(2):
+                for to_row in rows:
+                    send(out_f, in_f, ch, send_f, recv_f, to_row, to_sub)
+
+        return carry
+
+    lax.fori_loop(1, n_sub, later_class, 0)
+
+    @pl.when(jnp.logical_not(late))
     def _():
-        pl.semaphore_wait(here_sem, 1)
+        pl.semaphore_wait(here_sem.at[n_sub], 1)
         for ch in range(2):
             send(out_f, in_f, ch, send_f, recv_f, 0, 0)
 
@@ -351,7 +365,8 @@
                 flat(out_b)[pl.ds(4 * ch + 2 * part + tile, devices, stride=8), :] = grid[
                     devices * part : devices * (part + 1), LANES * tile : LANES * (tile + 1)
                 ]
-        send_all(out_b, in_b, ch, send_b, recv_b, True)
+        each_peer(functools.partial(send, out_b, in_b, ch, send_b, recv_b))
+        keep_own(out_b, in_b, ch)
         return carry
 
     lax.fori_loop(0, 2, columns, 0)
@@ -464,9 +479,11 @@
             vmem((wide, wide), F32), vmem((2 * low_len, wide), F32),
             vmem((2 * low_len, wide), BF16), vmem((2 * low_len, wide), BF16),
             vmem((2 * low_len, wide), BF16), vmem((2 * low_len, wide), BF16),
-            sems((6,)), sems, sems((2,)), sems((2,)), sems((2,)), sems((2,)), sems, sems, pltpu.SemaphoreType.REGULAR,
+            sems((6,)), sems, sems((2,)), sems((2,)), sems((2,)), sems((2,)), sems, sems, pltpu.SemaphoreType.REGULAR((n_sub + 1,)),
         ],
-        compiler_params=pltpu.CompilerParams(collective_id=0, has_side_effects=True),
+        compiler_params=pltpu.CompilerParams(
+            collective_id=0, has_side_effects=True, vmem_limit_bytes=VMEM_LIMIT
+        ),
         name="cg_step",
     )(noise_var, residual_in, direction, spectrum.T, *(jnp.asarray(t) for t in (consts, turn_col, turn_row)))
     return pl.pallas_call(
@@ -478,6 +495,7 @@
         ),
         in_specs=[vmem_spec] * 4,
         out_specs=(vmem_spec, vmem_spec, smem_spec),
+        compiler_params=pltpu.CompilerParams(vmem_limit_bytes=VMEM_LIMIT),
         name="finish",
     )(total, residual_in, direction, image)
 

time: 63.4 us -> 64.4 us (1.016)
  Pallas kernels: 62 us -> 63 us
    pallas_call x1, Pallas kernels: 59.9 us -> 60.9 us  [body(): pl.pallas_call(functools.partial(kernel, n_row, n_sub, 1.0 / (embed * emb...]
where the time goes in v4:
time: 64.4 us; the launch traced here: 64.3 us
  Pallas kernels  63 us (98%)
  between operations  1.28 us (2%)
    pallas_call x1, Pallas kernels, body(): pl.pallas_call(functools.partial(kernel, n_row, n_sub, 1.0 / (embed * emb...  60.9 us
    pallas_call x1, Pallas kernels, body(): pl.pallas_call(finish, out_shape=(jax.ShapeDtypeStruct(block, F32), jax.S...  2.1 us

profile of v4, /device:TPU:513, one launch (start us, length us, event | category | flops | bytes accessed | tf_op | source)
XLA Modules:
  0.0 64.3 jit_solution(15761320265939396511)
XLA Ops:
  1.3 60.9 %cg_step.1 = (f32[2,16,2048]{2,1,0:T(8,128)}, f32[1,128]{1,0:T(1,128)}) custom-call(f32[1]{0:T(128)S(6)} %copy.10.noise_ref, f32[2,16,2048]{2,1,0:T(8,128)} %resid.1, f32[2,16,2048]{2,1,0:T(8,128)} %direct.1, f32[32,4096]{1,0:T(8,128)} %bitcast.1, bf16[2,2048,256]{2,1,0:T(8,128)(2,1)} %constant.6.clone.consts_hbm, ...), custom_call_target="tpu_custom_call" | custom-call | tf_op jit(solution)/shard_map/cg_step/pallas_call | solution.py:469
  62.2 2.1 %finish.1 = (f32[2,16,2048]{2,1,0:T(8,128)}, f32[2,16,2048]{2,1,0:T(8,128)}, f32[2]{0:T(128)}) custom-call(f32[1,128]{1,0:T(1,128)} %get-tuple-element.5.total_ref, f32[2,16,2048]{2,1,0:T(8,128)} %resid.1, f32[2,16,2048]{2,1,0:T(8,128)} %direct.1, f32[2,16,2048]{2,1,0:T(8,128)} %get-tuple-element.6.image), custom_call_target="tpu_custom_call" | custom-call | tf_op jit(solution)/shard_map/finish/pallas_call | solution.py:489

commit v5 on v3

--- a/solution.py
+++ b/solution.py
@@ -13,6 +13,7 @@
 ROW_SUB = ("row", "sub")
 MESH = pl.DeviceIdType.MESH
 TINY = 1e-06
+VMEM_LIMIT = 107 << 19
 LANES = 128
 RADIX = 16
 F32 = jnp.float32
@@ -66,8 +67,8 @@
             odd = np.exp(-2j * np.pi * e * ch / (2 * RADIX))
             turn_row[ch, RADIX + e, 0] = odd.real
             turn_row[ch, RADIX + e, 1] = odd.imag
-    turn_row = turn_row.reshape(2, 4 * RADIX, LANES).astype(np.float32)
-    return consts, turn_col, turn_row
+    turns = np.concatenate([turn_row.reshape(-1, LANES), turn_col.reshape(-1, LANES)]).astype(np.float32)
+    return consts, turns
 
 
 def add(x, y):
@@ -146,19 +147,19 @@
 
 def kernel(
     n_row, n_sub, scale,
-    noise_ref, resid_hbm, dir_hbm, spec_hbm, consts_hbm, turn_col_hbm, turn_row_hbm,
-    image_out, total_out,
-    resid, direct, spec, consts, turn_col, turn_row,
-    out_f, in_f, out_b, in_b, sums, spec_t, image,
+    noise_ref, resid_hbm, dir_hbm, spec_hbm, consts_hbm, turns_hbm,
+    image, total_out,
+    resid, direct, spec, consts, turns,
+    out_f, in_f, out_b, in_b, sums, spec_t,
     work, tall, left_hi, left_lo, right_hi, right_lo,
-    load_sem, store_sem, send_f, recv_f, send_b, recv_b, send_s, recv_s, here_sem,
+    load_sem, send_f, recv_f, send_b, recv_b, send_s, recv_s, here_sem,
 ):
     devices = n_row * n_sub
     row, sub_ = lax.axis_index("row"), lax.axis_index("sub")
     me = row * n_sub + sub_
     offsets = far_first(n_row, n_sub)
     wide = 2 * LANES
-    low_len = turn_col.shape[1]
+    low_len = tall.shape[0] // 2
 
     def load(src, dst, slot):
         copy = pltpu.make_async_copy(src, dst, load_sem.at[slot])
@@ -185,6 +186,7 @@
         for to_sub in subs[:-1]:
             act(row, to_sub)
 
+    loads = [load(dir_hbm, direct, 0), load(turns_hbm, turns, 1), load(consts_hbm, consts, 2)]
     barrier = pltpu.get_barrier_semaphore()
 
     def greet(to_row, to_sub):
@@ -197,14 +199,9 @@
     def _():
         each_peer(greet)
 
-    loads = [
-        load(dir_hbm, direct, 0),
-        load(turn_row_hbm, turn_row, 1),
-        load(consts_hbm, consts, 2),
-        load(turn_col_hbm, turn_col, 3),
-        load(resid_hbm, resid, 4),
-    ]
-    loads += [load(spec_hbm.at[:, pl.ds(LANES * t, LANES)], spec.at[t], 5) for t in range(spec.shape[0])]
+    load(resid_hbm, resid, 3)
+    for t in range(spec.shape[0]):
+        load(spec_hbm.at[:, pl.ds(LANES * t, LANES)], spec.at[t], 4)
 
     def const(index, count=1):
         rows = pl.ds(wide * index, wide * count)
@@ -240,12 +237,15 @@
         return ref.reshape(devices * 8, LANES)
 
     def turn(ch, index):
-        both = turn_row[ch, pl.ds(2 * index, 2), :]
+        both = turns[pl.ds(4 * RADIX * ch + 2 * index, 2), :]
         return both[0:1], both[1:2]
 
-    loads[0].wait()
-    loads[1].wait()
-    loads[2].wait()
+    def turn_col(at, step):
+        first = 8 * RADIX + at
+        return turns[pl.ds(first, step), :], turns[pl.ds(first + low_len, step), :]
+
+    for copy in loads:
+        copy.wait()
 
     def rows_forward(ch, carry):
         for top in range(2):
@@ -281,9 +281,8 @@
 
     lax.fori_loop(0, 2, rows_forward, 0)
 
-    for copy in loads[3:5]:
-        copy.wait()
-    pltpu.make_async_copy(spec, spec, load_sem.at[5]).wait()
+    pltpu.make_async_copy(resid, resid, load_sem.at[3]).wait()
+    pltpu.make_async_copy(spec, spec, load_sem.at[4]).wait()
     spec_rows = spec.reshape(spec.shape[0] * spec.shape[1], LANES)
     for ch in range(2):
         for tile in range(2):
@@ -318,7 +317,7 @@
                 lines = pl.ds(at, step)
                 value = times(
                     (tall[lines, lanes], tall[pl.ds(low_len + at, step), lanes]),
-                    (turn_col[0, lines, :], turn_col[1, lines, :]),
+                    turn_col(at, step),
                 )
                 for part in range(2):
                     here = (pl.ds(low_len * tile + at, step), pl.ds(LANES * part, LANES))
@@ -337,7 +336,7 @@
                 here = pl.ds(low_len * tile + at, step)
                 value = times_conj(
                     (tall[here, pl.ds(0, LANES)], tall[here, pl.ds(LANES, LANES)]),
-                    (turn_col[0, lines, :], turn_col[1, lines, :]),
+                    turn_col(at, step),
                 )
                 for part in range(2):
                     there = (pl.ds(low_len * part + at, step), pl.ds(LANES * tile, LANES))
@@ -383,8 +382,6 @@
         return carry
 
     lax.fori_loop(0, 2, rows_back, 0)
-    leave = pltpu.make_async_copy(image, image_out, store_sem)
-    leave.start()
 
     def sum_rows(value):
         return jnp.sum(value, axis=0, keepdims=True)
@@ -419,7 +416,6 @@
     pltpu.make_async_copy(others, others, send_s).wait()
     pltpu.make_async_copy(others, others, recv_s).wait()
     total_out[...] = jnp.sum(sums[...], axis=0)
-    leave.wait()
 
 
 def finish(total_ref, resid, direct, image, resid_out, dir_out, step_out):
@@ -441,7 +437,7 @@
     probes, rows_dev, grid_len = direction.shape
     devices = n_row * n_sub
     embed = 2 * grid_len
-    consts, turn_col, turn_row = tables(rows_dev, grid_len, devices)
+    consts, turns = tables(rows_dev, grid_len, devices)
     low_len = embed // RADIX
     wide = 2 * LANES
     slots = (devices, 8, LANES)
@@ -454,21 +450,23 @@
     image, total = pl.pallas_call(
         functools.partial(kernel, n_row, n_sub, 1.0 / (embed * embed)),
         out_shape=(jax.ShapeDtypeStruct(block, F32), jax.ShapeDtypeStruct((1, LANES), F32)),
-        in_specs=[smem_spec] + [hbm_spec] * 6,
-        out_specs=(hbm_spec, vmem_spec),
+        in_specs=[smem_spec] + [hbm_spec] * 5,
+        out_specs=(vmem_spec, vmem_spec),
         scratch_shapes=[
             vmem(block, F32), vmem(block, F32), vmem((embed // LANES, spectrum.shape[1], LANES), F32),
-            vmem(consts.shape, BF16), vmem(turn_col.shape, F32), vmem(turn_row.shape, F32),
+            vmem(consts.shape, BF16), vmem(turns.shape, F32),
             vmem(slots, F32), vmem(slots, F32), vmem(slots, F32), vmem(slots, F32),
-            vmem((devices, 1, LANES), F32), vmem((low_len, 4 * LANES), F32), vmem(block, F32),
+            vmem((devices, 1, LANES), F32), vmem((low_len, 4 * LANES), F32),
             vmem((wide, wide), F32), vmem((2 * low_len, wide), F32),
             vmem((2 * low_len, wide), BF16), vmem((2 * low_len, wide), BF16),
             vmem((2 * low_len, wide), BF16), vmem((2 * low_len, wide), BF16),
-            sems((6,)), sems, sems((2,)), sems((2,)), sems((2,)), sems((2,)), sems, sems, pltpu.SemaphoreType.REGULAR,
+            sems((5,)), sems((2,)), sems((2,)), sems((2,)), sems((2,)), sems, sems, pltpu.SemaphoreType.REGULAR,
         ],
-        compiler_params=pltpu.CompilerParams(collective_id=0, has_side_effects=True),
+        compiler_params=pltpu.CompilerParams(
+            collective_id=0, has_side_effects=True, vmem_limit_bytes=VMEM_LIMIT
+        ),
         name="cg_step",
-    )(noise_var, residual_in, direction, spectrum.T, *(jnp.asarray(t) for t in (consts, turn_col, turn_row)))
+    )(noise_var, residual_in, direction, spectrum.T, *(jnp.asarray(t) for t in (consts, turns)))
     return pl.pallas_call(
         finish,
         out_shape=(
@@ -478,6 +476,7 @@
         ),
         in_specs=[vmem_spec] * 4,
         out_specs=(vmem_spec, vmem_spec, smem_spec),
+        compiler_params=pltpu.CompilerParams(vmem_limit_bytes=8 << 20),
         name="finish",
     )(total, residual_in, direction, image)
 

time: 63.4 us -> 61.5 us (0.970)
  Pallas kernels: 62 us -> 60 us
    pallas_call x1, Pallas kernels: 2.1 us -> 0.99 us  [body(): pl.pallas_call(finish, out_shape=(jax.ShapeDtypeStruct(block, F32), jax.S...]
    pallas_call x1, Pallas kernels: 59.9 us -> 59 us  [body(): pl.pallas_call(functools.partial(kernel, n_row, n_sub, 1.0 / (embed * emb...]
where the time goes in v5:
time: 61.5 us; the launch traced here: 61.4 us
  Pallas kernels  60 us (98%)
  between operations  1.37 us (2%)
    pallas_call x1, Pallas kernels, body(): pl.pallas_call(functools.partial(kernel, n_row, n_sub, 1.0 / (embed * emb...  59 us

profile of v5, /device:TPU:513, one launch (start us, length us, event | category | flops | bytes accessed | tf_op | source)
XLA Modules:
  0.0 61.4 jit_solution(11728106637025187520)
XLA Ops:
  0.6 0.0 copy-start.1
  0.6 0.0 copy-start
  1.4 59.0 %cg_step.1 = (f32[2,16,2048]{2,1,0:T(8,128)S(1)}, f32[1,128]{1,0:T(1,128)S(1)}) custom-call(f32[1]{0:T(128)S(6)} %copy.9.noise_ref, f32[2,16,2048]{2,1,0:T(8,128)} %resid.1, f32[2,16,2048]{2,1,0:T(8,128)} %direct.1, f32[32,4096]{1,0:T(8,128)} %bitcast.1, bf16[2,2048,256]{2,1,0:T(8,128)(2,1)} %constant.4.clone.consts_hbm, f32[640,128]{1,0:T(8,128)} %constant.5.clone.turns_hbm), custom_call_target="tpu_custom_call" | custom-call | tf_op jit(solution)/shard_map/cg_step/pallas_call | solution.py:450
  60.4 0.0 copy-done.1
  60.4 0.0 copy-done
  60.4 1.0 %finish.1 = (f32[2,16,2048]{2,1,0:T(8,128)}, f32[2,16,2048]{2,1,0:T(8,128)}, f32[2]{0:T(128)}) custom-call(f32[1,128]{1,0:T(1,128)S(1)} %get-tuple-element.5.total_ref, f32[2,16,2048]{2,1,0:T(8,128)S(1)} %copy-done, f32[2,16,2048]{2,1,0:T(8,128)S(1)} %copy-done.1, f32[2,16,2048]{2,1,0:T(8,128)S(1)} %get-tuple-element.6.image), custom_call_target="tpu_custom_call" | custom-call | tf_op jit(solution)/shard_map/finish/pallas_call | solution.py:470
Async XLA Ops:
  0.6 59.7 %copy-start.1 = (f32[2,16,2048]{2,1,0:T(8,128)S(1)}, f32[2,16,2048]{2,1,0:T(8,128)}, u32[]{:S(2)}) copy-start(f32[2,16,2048]{2,1,0:T(8,128)} %direct.1) | copy-start | bytes 786436
  0.6 59.7 %copy-start = (f32[2,16,2048]{2,1,0:T(8,128)S(1)}, f32[2,16,2048]{2,1,0:T(8,128)}, u32[]{:S(2)}) copy-start(f32[2,16,2048]{2,1,0:T(8,128)} %resid.1) | copy-start | bytes 786436

commit v6 on v5

--- a/solution.py
+++ b/solution.py
@@ -132,15 +132,6 @@
     )
 
 
-def far_first(n_row, n_sub):
-    def chips(row, sub_):
-        hop = row // 2
-        return min(hop, n_row // 2 - hop) + min(sub_, n_sub - sub_)
-
-    offsets = [(i, j) for i in range(n_row) for j in range(n_sub)][1:]
-    return sorted(offsets, key=lambda pair: -chips(*pair))
-
-
 def outward(count):
     return [count // 2 + (1 - 2 * (t % 2)) * ((t + 1) // 2) for t in range(count)]
 
@@ -157,7 +148,6 @@
     devices = n_row * n_sub
     row, sub_ = lax.axis_index("row"), lax.axis_index("sub")
     me = row * n_sub + sub_
-    offsets = far_first(n_row, n_sub)
     wide = 2 * LANES
     low_len = tall.shape[0] // 2
 
@@ -169,22 +159,18 @@
     def wrap(value, count):
         return jnp.where(value >= count, value - count, value)
 
-    def peer(i, j):
-        return wrap(row + i, n_row), wrap(sub_ + j, n_sub)
-
-    subs = [wrap(sub_ + j, n_sub) for j in outward(n_sub)]
+    rows = [wrap(row + i, n_row) for i in outward(n_row)]
 
     def each_peer(act):
-        def one_row(t, carry):
-            half = n_row // 2
-            to_row = wrap(row + half + (1 - 2 * (t % 2)) * ((t + 1) // 2), n_row)
-            for to_sub in subs:
+        def one_sub(t, carry):
+            to_sub = wrap(sub_ + n_sub // 2 + (1 - 2 * (t % 2)) * ((t + 1) // 2), n_sub)
+            for to_row in rows:
                 act(to_row, to_sub)
             return carry
 
-        lax.fori_loop(0, n_row - 1, one_row, 0)
-        for to_sub in subs[:-1]:
-            act(row, to_sub)
+        lax.fori_loop(0, n_sub - 1, one_sub, 0)
+        for to_row in rows[:-1]:
+            act(to_row, sub_)
 
     loads = [load(dir_hbm, direct, 0), load(turns_hbm, turns, 1), load(consts_hbm, consts, 2)]
     barrier = pltpu.get_barrier_semaphore()
@@ -207,31 +193,33 @@
         rows = pl.ds(wide * index, wide * count)
         return consts[0, rows, :], consts[1, rows, :]
 
-    def send(src, dst, ch, send_sem, recv_sem, to_row, to_sub):
-        part = pl.ds(4 * ch, 4)
+    def lines_of(piece):
+        return pl.ds(2 * piece, 4 if isinstance(piece, int) and piece == 2 else 2)
+
+    def send(src, dst, piece, send_sem, recv_sem, to_row, to_sub):
         pltpu.make_async_remote_copy(
-            src.at[to_row * n_sub + to_sub, part],
-            dst.at[me, part],
-            send_sem.at[ch],
-            recv_sem.at[ch],
+            src.at[to_row * n_sub + to_sub, lines_of(piece)],
+            dst.at[me, lines_of(piece)],
+            send_sem.at[piece],
+            recv_sem.at[piece],
             device_id={"row": to_row, "sub": to_sub},
             device_id_type=MESH,
         ).start()
 
-    def send_all(src, dst, ch, send_sem, recv_sem, all_here):
-        for i, j in offsets:
-            to_row, to_sub = peer(i, j)
-            go = functools.partial(send, src, dst, ch, send_sem, recv_sem, to_row, to_sub)
+    def send_all(src, dst, piece, send_sem, recv_sem, all_here):
+        def act(to_row, to_sub):
+            go = functools.partial(send, src, dst, piece, send_sem, recv_sem, to_row, to_sub)
             if all_here:
                 go()
             else:
                 pl.when(to_row + to_sub != 0)(go)
-        part = pl.ds(4 * ch, 4)
-        dst[me, part] = src[me, part]
-
-    def wait_all(ref, ch, sem):
-        others = ref.at[pl.ds(0, devices - 1), pl.ds(4 * ch, 4)]
-        pltpu.make_async_copy(others, others, sem.at[ch]).wait()
+
+        each_peer(act)
+        dst[me, lines_of(piece)] = src[me, lines_of(piece)]
+
+    def wait_all(ref, piece, sem):
+        others = ref.at[pl.ds(0, devices - 1), lines_of(piece)]
+        pltpu.make_async_copy(others, others, sem.at[piece]).wait()
 
     def flat(ref):
         return ref.reshape(devices * 8, LANES)
@@ -247,7 +235,7 @@
     for copy in loads:
         copy.wait()
 
-    def rows_forward(ch, carry):
+    def rows_forward(ch):
         for top in range(2):
             lines = pl.ds(8 * top, 8)
             values = []
@@ -264,22 +252,20 @@
         freq = dot3(const(0), (right_hi[pl.ds(0, wide), :], right_lo[pl.ds(0, wide), :]), transposed=True)
         for part in range(2):
             for tile in range(2):
-                flat(out_f)[pl.ds(4 * ch + 2 * part + tile, devices, stride=8), :] = freq[
+                flat(out_f)[pl.ds(4 * ch + 2 * tile + part, devices, stride=8), :] = freq[
                     devices * part : devices * (part + 1), LANES * tile : LANES * (tile + 1)
                 ]
 
-        @pl.when(ch == 0)
-        def _():
-            pl.semaphore_wait(barrier, jnp.where(me == 0, devices - 1, devices - 2))
-
-            @pl.when(me == 0)
-            def _():
-                each_peer(announce)
-
-        send_all(out_f, in_f, ch, send_f, recv_f, False)
-        return carry
-
-    lax.fori_loop(0, 2, rows_forward, 0)
+    rows_forward(0)
+    pl.semaphore_wait(barrier, jnp.where(me == 0, devices - 1, devices - 2))
+
+    @pl.when(me == 0)
+    def _():
+        each_peer(announce)
+
+    lax.fori_loop(0, 2, lambda piece, carry: (send_all(out_f, in_f, piece, send_f, recv_f, False), carry)[1], 0)
+    rows_forward(1)
+    send_all(out_f, in_f, 2, send_f, recv_f, False)
 
     pltpu.make_async_copy(resid, resid, load_sem.at[3]).wait()
     pltpu.make_async_copy(spec, spec, load_sem.at[4]).wait()
@@ -298,72 +284,69 @@
     @pl.when(me != 0)
     def _():
         pl.semaphore_wait(here_sem, 1)
-        for ch in range(2):
-            send(out_f, in_f, ch, send_f, recv_f, 0, 0)
-
-    def columns(ch, carry):
-        wait_all(in_f, ch, recv_f)
+        for piece in range(3):
+            send(out_f, in_f, piece, send_f, recv_f, 0, 0)
+
+    def columns(ch, piece, first_tile, tiles):
+        wait_all(in_f, piece, recv_f)
+        width = LANES * tiles
+        count = low_len * tiles
+        step = 32
         for part in range(2):
-            for tile in range(2):
+            for tile in range(tiles):
                 here = (pl.ds(devices * part, devices), pl.ds(LANES * tile, LANES))
                 right_hi[here], right_lo[here] = split(
-                    flat(in_f)[pl.ds(4 * ch + 2 * part + tile, devices, stride=8), :]
+                    flat(in_f)[pl.ds(4 * ch + 2 * (first_tile + tile) + part, devices, stride=8), :]
                 )
-        tall[...] = dot3(const(1, 2), (right_hi[pl.ds(0, wide), :], right_lo[pl.ds(0, wide), :]))
-        step = 32
-        for tile in range(2):
+        operand = (pl.ds(0, wide), pl.ds(0, width))
+        tall[:, pl.ds(0, width)] = dot3(const(1, 2), (right_hi[operand], right_lo[operand]))
+        for tile in range(tiles):
             lanes = pl.ds(LANES * tile, LANES)
             for at in range(0, low_len, step):
                 lines = pl.ds(at, step)
-                value = times(
-                    (tall[lines, lanes], tall[pl.ds(low_len + at, step), lanes]),
-                    turn_col(at, step),
-                )
+                value = times((tall[lines, lanes], tall[pl.ds(low_len + at, step), lanes]), turn_col(at, step))
                 for part in range(2):
                     here = (pl.ds(low_len * tile + at, step), pl.ds(LANES * part, LANES))
                     left_hi[here], left_lo[here] = split(value[part])
-        tall[...] = dot3((left_hi[...], left_lo[...]), const(3))
-        for tile in range(2):
+        used = pl.ds(0, count)
+        tall[used, :] = dot3((left_hi[used, :], left_lo[used, :]), const(3))
+        for tile in range(tiles):
+            lanes = pl.ds(pl.multiple_of(wide * ch + LANES * (first_tile + tile), LANES), LANES)
             for at in range(0, low_len, step):
-                weight = spec_t[pl.ds(at, step), pl.ds(pl.multiple_of(wide * ch + LANES * tile, LANES), LANES)]
+                weight = spec_t[pl.ds(at, step), lanes]
                 for part in range(2):
                     here = (pl.ds(low_len * tile + at, step), pl.ds(LANES * part, LANES))
                     left_hi[here], left_lo[here] = split(tall[here] * weight)
-        tall[...] = dot3((left_hi[...], left_lo[...]), const(4))
-        for tile in range(2):
+        tall[used, :] = dot3((left_hi[used, :], left_lo[used, :]), const(4))
+        for tile in range(tiles):
             for at in range(0, low_len, step):
-                lines = pl.ds(at, step)
                 here = pl.ds(low_len * tile + at, step)
-                value = times_conj(
-                    (tall[here, pl.ds(0, LANES)], tall[here, pl.ds(LANES, LANES)]),
-                    turn_col(at, step),
-                )
+                value = times_conj((tall[here, pl.ds(0, LANES)], tall[here, pl.ds(LANES, LANES)]), turn_col(at, step))
                 for part in range(2):
                     there = (pl.ds(low_len * part + at, step), pl.ds(LANES * tile, LANES))
                     right_hi[there], right_lo[there] = split(value[part])
-        low, high = pl.ds(0, low_len), pl.ds(low_len, low_len)
-        grid = dot3(const(5), (right_hi[low, :], right_lo[low, :])) + dot3(
-            const(6), (right_hi[high, :], right_lo[high, :])
-        )
+        low, high = (pl.ds(0, low_len), pl.ds(0, width)), (pl.ds(low_len, low_len), pl.ds(0, width))
+        grid = dot3(const(5), (right_hi[low], right_lo[low])) + dot3(const(6), (right_hi[high], right_lo[high]))
         for part in range(2):
-            for tile in range(2):
-                flat(out_b)[pl.ds(4 * ch + 2 * part + tile, devices, stride=8), :] = grid[
+            for tile in range(tiles):
+                flat(out_b)[pl.ds(4 * ch + 2 * (first_tile + tile) + part, devices, stride=8), :] = grid[
                     devices * part : devices * (part + 1), LANES * tile : LANES * (tile + 1)
                 ]
-        send_all(out_b, in_b, ch, send_b, recv_b, True)
-        return carry
-
-    lax.fori_loop(0, 2, columns, 0)
+        send_all(out_b, in_b, piece, send_b, recv_b, True)
+
+    lax.fori_loop(0, 2, lambda piece, carry: (columns(0, piece, piece, 1), carry)[1], 0)
+    columns(1, 2, 0, 2)
 
     noise = noise_ref[0]
     image[...] = noise * direct[...]
 
-    def rows_back(ch, carry):
-        wait_all(in_b, ch, recv_b)
+    def rows_back(ch):
+        for piece in ((0, 1), (2,))[ch]:
+            wait_all(in_b, piece, recv_b)
         for part in range(2):
             for tile in range(2):
                 here = (pl.ds(LANES * tile, LANES), pl.ds(devices * part, devices))
-                block = flat(in_b)[pl.ds(4 * ch + 2 * part + tile, devices, stride=8), :]
+                block = flat(in_b)[pl.ds(4 * ch + 2 * tile + part, devices, stride=8), :]
                 left_hi[here], left_lo[here] = split(block.T)
         work[...] = dot3((left_hi[pl.ds(0, wide), :], left_lo[pl.ds(0, wide), :]), const(7))
         for top in range(2):
@@ -379,9 +362,9 @@
                 lanes = pl.ds(LANES * a, LANES)
                 for part in range(2):
                     image[part, lines, lanes] += value[part]
-        return carry
-
-    lax.fori_loop(0, 2, rows_back, 0)
+
+    rows_back(0)
+    rows_back(1)
 
     def sum_rows(value):
         return jnp.sum(value, axis=0, keepdims=True)
@@ -409,9 +392,9 @@
         ).start()
 
     each_peer(tell)
-    for ch in range(2):
-        wait_all(out_f, ch, send_f)
-        wait_all(out_b, ch, send_b)
+    for piece in range(3):
+        wait_all(out_f, piece, send_f)
+        wait_all(out_b, piece, send_b)
     others = sums.at[pl.ds(0, devices - 1)]
     pltpu.make_async_copy(others, others, send_s).wait()
     pltpu.make_async_copy(others, others, recv_s).wait()
@@ -460,7 +443,7 @@
             vmem((wide, wide), F32), vmem((2 * low_len, wide), F32),
             vmem((2 * low_len, wide), BF16), vmem((2 * low_len, wide), BF16),
             vmem((2 * low_len, wide), BF16), vmem((2 * low_len, wide), BF16),
-            sems((5,)), sems((2,)), sems((2,)), sems((2,)), sems((2,)), sems, sems, pltpu.SemaphoreType.REGULAR,
+            sems((5,)), sems((3,)), sems((3,)), sems((3,)), sems((3,)), sems, sems, pltpu.SemaphoreType.REGULAR,
         ],
         compiler_params=pltpu.CompilerParams(
             collective_id=0, has_side_effects=True, vmem_limit_bytes=VMEM_LIMIT

time: 61.5 us -> 69.9 us (1.14)
  Pallas kernels: 60 us -> 68.3 us
    pallas_call x1, Pallas kernels: 59 us -> 67.4 us  [body(): pl.pallas_call(functools.partial(kernel, n_row, n_sub, 1.0 / (embed * emb...]
where the time goes in v6:
time: 69.9 us; the launch traced here: 69.7 us
  Pallas kernels  68.3 us (98%)
  between operations  1.37 us (2%)
    pallas_call x1, Pallas kernels, body(): pl.pallas_call(functools.partial(kernel, n_row, n_sub, 1.0 / (embed * emb...  67.4 us

profile of v6, /device:TPU:513, one launch (start us, length us, event | category | flops | bytes accessed | tf_op | source)
XLA Modules:
  0.0 69.7 jit_solution(15100116179426965091)
XLA Ops:
  0.6 0.0 copy-start.1
  0.6 0.0 copy-start
  1.4 67.4 %cg_step.1 = (f32[2,16,2048]{2,1,0:T(8,128)S(1)}, f32[1,128]{1,0:T(1,128)S(1)}) custom-call(f32[1]{0:T(128)S(6)} %copy.9.noise_ref, f32[2,16,2048]{2,1,0:T(8,128)} %resid.1, f32[2,16,2048]{2,1,0:T(8,128)} %direct.1, f32[32,4096]{1,0:T(8,128)} %bitcast.1, bf16[2,2048,256]{2,1,0:T(8,128)(2,1)} %constant.4.clone.consts_hbm, f32[640,128]{1,0:T(8,128)} %constant.5.clone.turns_hbm), custom_call_target="tpu_custom_call" | custom-call | tf_op jit(solution)/shard_map/cg_step/pallas_call | solution.py:433
  68.7 0.0 copy-done.1
  68.7 0.0 copy-done
  68.7 1.0 %finish.1 = (f32[2,16,2048]{2,1,0:T(8,128)}, f32[2,16,2048]{2,1,0:T(8,128)}, f32[2]{0:T(128)}) custom-call(f32[1,128]{1,0:T(1,128)S(1)} %get-tuple-element.5.total_ref, f32[2,16,2048]{2,1,0:T(8,128)S(1)} %copy-done, f32[2,16,2048]{2,1,0:T(8,128)S(1)} %copy-done.1, f32[2,16,2048]{2,1,0:T(8,128)S(1)} %get-tuple-element.6.image), custom_call_target="tpu_custom_call" | custom-call | tf_op jit(solution)/shard_map/finish/pallas_call | solution.py:453
Async XLA Ops:
  0.6 68.1 %copy-start.1 = (f32[2,16,2048]{2,1,0:T(8,128)S(1)}, f32[2,16,2048]{2,1,0:T(8,128)}, u32[]{:S(2)}) copy-start(f32[2,16,2048]{2,1,0:T(8,128)} %direct.1) | copy-start | bytes 786436
  0.6 68.1 %copy-start = (f32[2,16,2048]{2,1,0:T(8,128)S(1)}, f32[2,16,2048]{2,1,0:T(8,128)}, u32[]{:S(2)}) copy-start(f32[2,16,2048]{2,1,0:T(8,128)} %resid.1) | copy-start | bytes 786436

commit v7 on v5

--- a/solution.py
+++ b/solution.py
@@ -173,6 +173,9 @@
         return wrap(row + i, n_row), wrap(sub_ + j, n_sub)
 
     subs = [wrap(sub_ + j, n_sub) for j in outward(n_sub)]
+    rows = [wrap(row + i, n_row) for i in outward(n_row)]
+    late = me == 0
+    level = jnp.where(late, n_sub, sub_)
 
     def each_peer(act):
         def one_row(t, carry):
@@ -193,11 +196,22 @@
         pl.semaphore_signal(barrier, inc=1, device_id={"row": to_row, "sub": to_sub}, device_id_type=MESH)
 
     def announce(to_row, to_sub):
-        pl.semaphore_signal(here_sem, inc=1, device_id={"row": to_row, "sub": to_sub}, device_id_type=MESH)
-
-    @pl.when(me != 0)
+        pl.semaphore_signal(here_sem.at[level], inc=1, device_id={"row": to_row, "sub": to_sub}, device_id_type=MESH)
+
+    def greet_sub(to_sub, carry):
+        @pl.when(to_sub > sub_)
+        def _():
+            for to_row in rows:
+                greet(to_row, to_sub)
+
+        return carry
+
+    @pl.when(jnp.logical_not(late))
     def _():
-        each_peer(greet)
+        for to_row in rows[:-1]:
+            greet(to_row, sub_)
+        lax.fori_loop(1, n_sub, greet_sub, 0)
+        pl.when(sub_ != 0)(lambda: greet(0, 0))
 
     load(resid_hbm, resid, 3)
     for t in range(spec.shape[0]):
@@ -225,7 +239,7 @@
             if all_here:
                 go()
             else:
-                pl.when(to_row + to_sub != 0)(go)
+                pl.when((to_row + to_sub != 0) & (to_sub <= level))(go)
         part = pl.ds(4 * ch, 4)
         dst[me, part] = src[me, part]
 
@@ -270,11 +284,13 @@
 
         @pl.when(ch == 0)
         def _():
-            pl.semaphore_wait(barrier, jnp.where(me == 0, devices - 1, devices - 2))
-
-            @pl.when(me == 0)
+            pl.semaphore_wait(barrier, jnp.where(late, devices - 1, n_row * (sub_ + 1) - 2))
+            pl.when(late)(lambda: each_peer(announce))
+
+            @pl.when(jnp.logical_not(late))
             def _():
-                each_peer(announce)
+                for to_sub in range(n_sub):
+                    pl.when((to_sub < sub_) & (row + to_sub != 0))(functools.partial(announce, row, to_sub))
 
         send_all(out_f, in_f, ch, send_f, recv_f, False)
         return carry
@@ -295,9 +311,22 @@
                     jnp.concatenate(parts, axis=0).T * scale
                 )
 
-    @pl.when(me != 0)
+    def later_class(t, carry):
+        ch, to_sub = t // n_sub, t % n_sub
+
+        @pl.when(to_sub > level)
+        def _():
+            pl.when(ch == 0)(lambda: pl.semaphore_wait(here_sem.at[to_sub], 1))
+            for to_row in rows:
+                send(out_f, in_f, ch, send_f, recv_f, to_row, to_sub)
+
+        return carry
+
+    lax.fori_loop(0, 2 * n_sub, later_class, 0)
+
+    @pl.when(jnp.logical_not(late))
     def _():
-        pl.semaphore_wait(here_sem, 1)
+        pl.semaphore_wait(here_sem.at[n_sub], 1)
         for ch in range(2):
             send(out_f, in_f, ch, send_f, recv_f, 0, 0)
 
@@ -460,7 +489,7 @@
             vmem((wide, wide), F32), vmem((2 * low_len, wide), F32),
             vmem((2 * low_len, wide), BF16), vmem((2 * low_len, wide), BF16),
             vmem((2 * low_len, wide), BF16), vmem((2 * low_len, wide), BF16),
-            sems((5,)), sems((2,)), sems((2,)), sems((2,)), sems((2,)), sems, sems, pltpu.SemaphoreType.REGULAR,
+            sems((5,)), sems((2,)), sems((2,)), sems((2,)), sems((2,)), sems, sems, pltpu.SemaphoreType.REGULAR((n_sub + 1,)),
         ],
         compiler_params=pltpu.CompilerParams(
             collective_id=0, has_side_effects=True, vmem_limit_bytes=VMEM_LIMIT

time: 61.5 us -> 60.4 us (0.982)
  Pallas kernels: 60 us -> 58.9 us
    pallas_call x1, Pallas kernels: 59 us -> 57.9 us  [body(): pl.pallas_call(functools.partial(kernel, n_row, n_sub, 1.0 / (embed * emb...]
where the time goes in v7:
time: 60.4 us; the launch traced here: 60.3 us
  Pallas kernels  58.9 us (98%)
  between operations  1.37 us (2%)
    pallas_call x1, Pallas kernels, body(): pl.pallas_call(functools.partial(kernel, n_row, n_sub, 1.0 / (embed * emb...  57.9 us

profile of v7, /device:TPU:513, one launch (start us, length us, event | category | flops | bytes accessed | tf_op | source)
XLA Modules:
  0.0 60.3 jit_solution(15856617711201123252)
XLA Ops:
  0.6 0.0 copy-start.1
  0.6 0.0 copy-start
  1.4 57.9 %cg_step.1 = (f32[2,16,2048]{2,1,0:T(8,128)S(1)}, f32[1,128]{1,0:T(1,128)S(1)}) custom-call(f32[1]{0:T(128)S(6)} %copy.9.noise_ref, f32[2,16,2048]{2,1,0:T(8,128)} %resid.1, f32[2,16,2048]{2,1,0:T(8,128)} %direct.1, f32[32,4096]{1,0:T(8,128)} %bitcast.1, bf16[2,2048,256]{2,1,0:T(8,128)(2,1)} %constant.4.clone.consts_hbm, f32[640,128]{1,0:T(8,128)} %constant.5.clone.turns_hbm), custom_call_target="tpu_custom_call" | custom-call | tf_op jit(solution)/shard_map/cg_step/pallas_call | solution.py:479
  59.3 0.0 copy-done.1
  59.3 0.0 copy-done
  59.3 1.0 %finish.1 = (f32[2,16,2048]{2,1,0:T(8,128)}, f32[2,16,2048]{2,1,0:T(8,128)}, f32[2]{0:T(128)}) custom-call(f32[1,128]{1,0:T(1,128)S(1)} %get-tuple-element.5.total_ref, f32[2,16,2048]{2,1,0:T(8,128)S(1)} %copy-done, f32[2,16,2048]{2,1,0:T(8,128)S(1)} %copy-done.1, f32[2,16,2048]{2,1,0:T(8,128)S(1)} %get-tuple-element.6.image), custom_call_target="tpu_custom_call" | custom-call | tf_op jit(solution)/shard_map/finish/pallas_call | solution.py:499
Async XLA Ops:
  0.6 58.6 %copy-start.1 = (f32[2,16,2048]{2,1,0:T(8,128)S(1)}, f32[2,16,2048]{2,1,0:T(8,128)}, u32[]{:S(2)}) copy-start(f32[2,16,2048]{2,1,0:T(8,128)} %direct.1) | copy-start | bytes 786436
  0.6 58.6 %copy-start = (f32[2,16,2048]{2,1,0:T(8,128)S(1)}, f32[2,16,2048]{2,1,0:T(8,128)}, u32[]{:S(2)}) copy-start(f32[2,16,2048]{2,1,0:T(8,128)} %resid.1) | copy-start | bytes 786436

commit v8 on v7

--- a/solution.py
+++ b/solution.py
@@ -174,7 +174,12 @@
 
     subs = [wrap(sub_ + j, n_sub) for j in outward(n_sub)]
     rows = [wrap(row + i, n_row) for i in outward(n_row)]
-    late = me == 0
+    apart = lax.axis_index("grp") == 0
+    late = apart & (me == 0)
+
+    def ordinary(to_row, to_sub):
+        return (to_row + to_sub != 0) | jnp.logical_not(apart)
+
     level = jnp.where(late, n_sub, sub_)
 
     def each_peer(act):
@@ -189,7 +194,12 @@
         for to_sub in subs[:-1]:
             act(row, to_sub)
 
-    loads = [load(dir_hbm, direct, 0), load(turns_hbm, turns, 1), load(consts_hbm, consts, 2)]
+    first, rest = pl.ds(0, wide), pl.ds(wide, consts.shape[1] - wide)
+    loads = [
+        load(dir_hbm, direct, 0),
+        load(turns_hbm.at[pl.ds(0, 8 * RADIX)], turns.at[pl.ds(0, 8 * RADIX)], 1),
+        load(consts_hbm.at[:, first], consts.at[:, first], 2),
+    ]
     barrier = pltpu.get_barrier_semaphore()
 
     def greet(to_row, to_sub):
@@ -211,9 +221,13 @@
         for to_row in rows[:-1]:
             greet(to_row, sub_)
         lax.fori_loop(1, n_sub, greet_sub, 0)
-        pl.when(sub_ != 0)(lambda: greet(0, 0))
-
-    load(resid_hbm, resid, 3)
+        pl.when(apart & (sub_ != 0))(lambda: greet(0, 0))
+
+    later_loads = [
+        load(consts_hbm.at[:, rest], consts.at[:, rest], 5),
+        load(turns_hbm.at[pl.ds(8 * RADIX, 2 * low_len)], turns.at[pl.ds(8 * RADIX, 2 * low_len)], 6),
+        load(resid_hbm, resid, 3),
+    ]
     for t in range(spec.shape[0]):
         load(spec_hbm.at[:, pl.ds(LANES * t, LANES)], spec.at[t], 4)
 
@@ -239,7 +253,7 @@
             if all_here:
                 go()
             else:
-                pl.when((to_row + to_sub != 0) & (to_sub <= level))(go)
+                pl.when(ordinary(to_row, to_sub) & (to_sub <= level))(go)
         part = pl.ds(4 * ch, 4)
         dst[me, part] = src[me, part]
 
@@ -257,6 +271,11 @@
     def turn_col(at, step):
         first = 8 * RADIX + at
         return turns[pl.ds(first, step), :], turns[pl.ds(first + low_len, step), :]
+
+    @pl.when(late)
+    def _():
+        pl.semaphore_wait(barrier, devices - 1)
+        each_peer(announce)
 
     for copy in loads:
         copy.wait()
@@ -284,20 +303,19 @@
 
         @pl.when(ch == 0)
         def _():
-            pl.semaphore_wait(barrier, jnp.where(late, devices - 1, n_row * (sub_ + 1) - 2))
-            pl.when(late)(lambda: each_peer(announce))
-
             @pl.when(jnp.logical_not(late))
             def _():
+                pl.semaphore_wait(barrier, n_row * (sub_ + 1) - 1 - apart.astype(jnp.int32))
                 for to_sub in range(n_sub):
-                    pl.when((to_sub < sub_) & (row + to_sub != 0))(functools.partial(announce, row, to_sub))
+                    pl.when((to_sub < sub_) & ordinary(row, to_sub))(functools.partial(announce, row, to_sub))
 
         send_all(out_f, in_f, ch, send_f, recv_f, False)
         return carry
 
     lax.fori_loop(0, 2, rows_forward, 0)
 
-    pltpu.make_async_copy(resid, resid, load_sem.at[3]).wait()
+    for copy in later_loads:
+        copy.wait()
     pltpu.make_async_copy(spec, spec, load_sem.at[4]).wait()
     spec_rows = spec.reshape(spec.shape[0] * spec.shape[1], LANES)
     for ch in range(2):
@@ -324,7 +342,7 @@
 
     lax.fori_loop(0, 2 * n_sub, later_class, 0)
 
-    @pl.when(jnp.logical_not(late))
+    @pl.when(apart & jnp.logical_not(late))
     def _():
         pl.semaphore_wait(here_sem.at[n_sub], 1)
         for ch in range(2):
@@ -489,7 +507,7 @@
             vmem((wide, wide), F32), vmem((2 * low_len, wide), F32),
             vmem((2 * low_len, wide), BF16), vmem((2 * low_len, wide), BF16),
             vmem((2 * low_len, wide), BF16), vmem((2 * low_len, wide), BF16),
-            sems((5,)), sems((2,)), sems((2,)), sems((2,)), sems((2,)), sems, sems, pltpu.SemaphoreType.REGULAR((n_sub + 1,)),
+            sems((7,)), sems((2,)), sems((2,)), sems((2,)), sems((2,)), sems, sems, pltpu.SemaphoreType.REGULAR((n_sub + 1,)),
         ],
         compiler_params=pltpu.CompilerParams(
             collective_id=0, has_side_effects=True, vmem_limit_bytes=VMEM_LIMIT

time: 60.4 us -> 59.7 us (0.988)
  Pallas kernels: 58.9 us -> 58.2 us
    pallas_call x1, Pallas kernels: 57.9 us -> 57.3 us  [body(): pl.pallas_call(functools.partial(kernel, n_row, n_sub, 1.0 / (embed * emb...]
where the time goes in v8:
time: 59.7 us; the launch traced here: 59.6 us
  Pallas kernels  58.2 us (97%)
  between operations  1.37 us (2%)
    pallas_call x1, Pallas kernels, body(): pl.pallas_call(functools.partial(kernel, n_row, n_sub, 1.0 / (embed * emb...  57.3 us

profile of v8, /device:TPU:513, one launch (start us, length us, event | category | flops | bytes accessed | tf_op | source)
XLA Modules:
  0.0 59.6 jit_solution(413468867389065711)
XLA Ops:
  0.6 0.0 copy-start.1
  0.6 0.0 copy-start
  1.4 57.3 %cg_step.1 = (f32[2,16,2048]{2,1,0:T(8,128)S(1)}, f32[1,128]{1,0:T(1,128)S(1)}) custom-call(f32[1]{0:T(128)S(6)} %copy.9.noise_ref, f32[2,16,2048]{2,1,0:T(8,128)} %resid.1, f32[2,16,2048]{2,1,0:T(8,128)} %direct.1, f32[32,4096]{1,0:T(8,128)} %bitcast.1, bf16[2,2048,256]{2,1,0:T(8,128)(2,1)} %constant.4.clone.consts_hbm, f32[640,128]{1,0:T(8,128)} %constant.5.clone.turns_hbm), custom_call_target="tpu_custom_call" | custom-call | tf_op jit(solution)/shard_map/cg_step/pallas_call | solution.py:497
  58.6 0.0 copy-done.1
  58.6 0.0 copy-done
  58.6 1.0 %finish.1 = (f32[2,16,2048]{2,1,0:T(8,128)}, f32[2,16,2048]{2,1,0:T(8,128)}, f32[2]{0:T(128)}) custom-call(f32[1,128]{1,0:T(1,128)S(1)} %get-tuple-element.5.total_ref, f32[2,16,2048]{2,1,0:T(8,128)S(1)} %copy-done, f32[2,16,2048]{2,1,0:T(8,128)S(1)} %copy-done.1, f32[2,16,2048]{2,1,0:T(8,128)S(1)} %get-tuple-element.6.image), custom_call_target="tpu_custom_call" | custom-call | tf_op jit(solution)/shard_map/finish/pallas_call | solution.py:517
Async XLA Ops:
  0.6 58.0 %copy-start.1 = (f32[2,16,2048]{2,1,0:T(8,128)S(1)}, f32[2,16,2048]{2,1,0:T(8,128)}, u32[]{:S(2)}) copy-start(f32[2,16,2048]{2,1,0:T(8,128)} %direct.1) | copy-start | bytes 786436
  0.6 58.0 %copy-start = (f32[2,16,2048]{2,1,0:T(8,128)S(1)}, f32[2,16,2048]{2,1,0:T(8,128)}, u32[]{:S(2)}) copy-start(f32[2,16,2048]{2,1,0:T(8,128)} %resid.1) | copy-start | bytes 786436

commit v9 on v8

--- a/solution.py
+++ b/solution.py
@@ -455,7 +455,8 @@
             device_id={"row": to_row, "sub": to_sub}, device_id_type=MESH,
         ).start()
 
-    each_peer(tell)
+    for i, j in offsets:
+        tell(*peer(i, j))
     for ch in range(2):
         wait_all(out_f, ch, send_f)
         wait_all(out_b, ch, send_b)

time: 59.7 us -> 59.5 us (level)
  no operation moved by 1% of the time
where the time goes in v9:
time: 59.5 us; the launch traced here: 59.4 us
  Pallas kernels  58 us (97%)
  between operations  1.37 us (2%)
    pallas_call x1, Pallas kernels, body(): pl.pallas_call(functools.partial(kernel, n_row, n_sub, 1.0 / (embed * emb...  57 us

profile of v9, /device:TPU:513, one launch (start us, length us, event | category | flops | bytes accessed | tf_op | source)
XLA Modules:
  0.0 59.4 jit_solution(15169203443392470609)
XLA Ops:
  0.6 0.0 copy-start.1
  0.6 0.0 copy-start
  1.4 57.0 %cg_step.1 = (f32[2,16,2048]{2,1,0:T(8,128)S(1)}, f32[1,128]{1,0:T(1,128)S(1)}) custom-call(f32[1]{0:T(128)S(6)} %copy.9.noise_ref, f32[2,16,2048]{2,1,0:T(8,128)} %resid.1, f32[2,16,2048]{2,1,0:T(8,128)} %direct.1, f32[32,4096]{1,0:T(8,128)} %bitcast.1, bf16[2,2048,256]{2,1,0:T(8,128)(2,1)} %constant.4.clone.consts_hbm, f32[640,128]{1,0:T(8,128)} %constant.5.clone.turns_hbm), custom_call_target="tpu_custom_call" | custom-call | tf_op jit(solution)/shard_map/cg_step/pallas_call | solution.py:498
  58.4 0.0 copy-done.1
  58.4 0.0 copy-done
  58.4 1.0 %finish.1 = (f32[2,16,2048]{2,1,0:T(8,128)}, f32[2,16,2048]{2,1,0:T(8,128)}, f32[2]{0:T(128)}) custom-call(f32[1,128]{1,0:T(1,128)S(1)} %get-tuple-element.5.total_ref, f32[2,16,2048]{2,1,0:T(8,128)S(1)} %copy-done, f32[2,16,2048]{2,1,0:T(8,128)S(1)} %copy-done.1, f32[2,16,2048]{2,1,0:T(8,128)S(1)} %get-tuple-element.6.image), custom_call_target="tpu_custom_call" | custom-call | tf_op jit(solution)/shard_map/finish/pallas_call | solution.py:518
Async XLA Ops:
  0.6 57.7 %copy-start.1 = (f32[2,16,2048]{2,1,0:T(8,128)S(1)}, f32[2,16,2048]{2,1,0:T(8,128)}, u32[]{:S(2)}) copy-start(f32[2,16,2048]{2,1,0:T(8,128)} %direct.1) | copy-start | bytes 786436
  0.6 57.7 %copy-start = (f32[2,16,2048]{2,1,0:T(8,128)S(1)}, f32[2,16,2048]{2,1,0:T(8,128)}, u32[]{:S(2)}) copy-start(f32[2,16,2048]{2,1,0:T(8,128)} %resid.1) | copy-start | bytes 786436

commit v10 on v9

--- a/solution.py
+++ b/solution.py
@@ -170,7 +170,9 @@
         return jnp.where(value >= count, value - count, value)
 
     def peer(i, j):
-        return wrap(row + i, n_row), wrap(sub_ + j, n_sub)
+        hop, core = i // 2, row % 2
+        to_core = core if i % 2 == 0 else 1 - core
+        return 2 * wrap(row // 2 + hop, n_row // 2) + to_core, wrap(sub_ + j, n_sub)
 
     subs = [wrap(sub_ + j, n_sub) for j in outward(n_sub)]
     rows = [wrap(row + i, n_row) for i in outward(n_row)]

time: 59.5 us -> 59.4 us (level)
  no operation moved by 1% of the time
where the time goes in v10:
time: 59.4 us; the launch traced here: 59.3 us
  Pallas kernels  57.9 us (97%)
  between operations  1.37 us (2%)
    pallas_call x1, Pallas kernels, body(): pl.pallas_call(functools.partial(kernel, n_row, n_sub, 1.0 / (embed * emb...  56.9 us

profile of v10, /device:TPU:513, one launch (start us, length us, event | category | flops | bytes accessed | tf_op | source)
XLA Modules:
  0.0 59.3 jit_solution(16900754520542093157)
XLA Ops:
  0.6 0.0 copy-start.1
  0.6 0.0 copy-start
  1.4 56.9 %cg_step.1 = (f32[2,16,2048]{2,1,0:T(8,128)S(1)}, f32[1,128]{1,0:T(1,128)S(1)}) custom-call(f32[1]{0:T(128)S(6)} %copy.9.noise_ref, f32[2,16,2048]{2,1,0:T(8,128)} %resid.1, f32[2,16,2048]{2,1,0:T(8,128)} %direct.1, f32[32,4096]{1,0:T(8,128)} %bitcast.1, bf16[2,2048,256]{2,1,0:T(8,128)(2,1)} %constant.4.clone.consts_hbm, f32[640,128]{1,0:T(8,128)} %constant.5.clone.turns_hbm), custom_call_target="tpu_custom_call" | custom-call | tf_op jit(solution)/shard_map/cg_step/pallas_call | solution.py:500
  58.3 0.0 copy-done.1
  58.3 0.0 copy-done
  58.3 1.0 %finish.1 = (f32[2,16,2048]{2,1,0:T(8,128)}, f32[2,16,2048]{2,1,0:T(8,128)}, f32[2]{0:T(128)}) custom-call(f32[1,128]{1,0:T(1,128)S(1)} %get-tuple-element.5.total_ref, f32[2,16,2048]{2,1,0:T(8,128)S(1)} %copy-done, f32[2,16,2048]{2,1,0:T(8,128)S(1)} %copy-done.1, f32[2,16,2048]{2,1,0:T(8,128)S(1)} %get-tuple-element.6.image), custom_call_target="tpu_custom_call" | custom-call | tf_op jit(solution)/shard_map/finish/pallas_call | solution.py:520
Async XLA Ops:
  0.6 57.7 %copy-start.1 = (f32[2,16,2048]{2,1,0:T(8,128)S(1)}, f32[2,16,2048]{2,1,0:T(8,128)}, u32[]{:S(2)}) copy-start(f32[2,16,2048]{2,1,0:T(8,128)} %direct.1) | copy-start | bytes 786436
  0.6 57.7 %copy-start = (f32[2,16,2048]{2,1,0:T(8,128)S(1)}, f32[2,16,2048]{2,1,0:T(8,128)}, u32[]{:S(2)}) copy-start(f32[2,16,2048]{2,1,0:T(8,128)} %resid.1) | copy-start | bytes 786436
